TPU v7x, 8 devices: a whole 2x2x1 slice. The times are simulated.
8 devices in a mesh: dp: 1 (over z), tp: 2 (over y), cp: 4 (over x, core).
Axes of the slice: x: 2, y: 2, z: 1, core: 2. Of those that a mesh axis runs over, the one named last changes fastest.
Arguments:
- hidden: bfloat16 [2048, 8192], P(('dp', 'cp'))
- tok_pos: int32 [2048], P(('dp', 'cp'))
- norm_gain: float32 [8192], replicated
- w_query: bfloat16 [8192, 8192], P(None, 'tp')
- w_key: bfloat16 [8192, 1024], P(None, 'tp')
- w_value: bfloat16 [8192, 1024], P(None, 'tp')
- w_out: bfloat16 [8192, 8192], P('tp')
Outputs:
- output 1: bfloat16 [2048, 8192], P(('dp', 'cp'))
- output 2: bfloat16 [2048, 8, 128], P(('dp', 'cp'), 'tp')
- output 3: bfloat16 [2048, 8, 128], P(('dp', 'cp'), 'tp')
All inputs are finite; a program needn't handle non-finite values.
Results may differ from a plain program's by a relative error of at most 0.00490281.
Values are sent between devices in bfloat16 or wider.
A program may use at most 1 GiB of HBM per device.

v0:
```python
import functools

import jax
import jax.numpy as jnp
from jax import lax
from jax.experimental import pallas as pl
from jax.experimental.pallas import tpu as pltpu
from jax.sharding import PartitionSpec as P


HEAD = 128
THETA = 1000000
EPS = 1e-5
NEG_BIG = -1e30
EXP_SCALE = HEAD ** -0.5 * 1.4426950408889634
Q_ROWS = 128
PAIR = 2
STEP = 256
SLOTS = 8
CUTS = (0, 1024, 3072, 5120, 7168, 8192)
ANY = pl.BlockSpec(memory_space=pl.ANY)
VMEM = pl.BlockSpec(memory_space=pltpu.VMEM)
MESH = pl.DeviceIdType.MESH


def dot(a, b):
    return jnp.dot(a, b, preferred_element_type=jnp.float32)


def rope_rows():
    half = HEAD // 2
    inv_freq = 1.0 / (THETA ** ((2 * (jnp.arange(HEAD) % half)).astype(jnp.float32) / HEAD))
    return jnp.stack([inv_freq, jnp.where(jnp.arange(HEAD) < half, -1.0, 1.0)])


def rotate(x, cos, sin):
    return (x * cos + pltpu.roll(x, HEAD // 2, 1) * sin).astype(jnp.bfloat16)


def front_kernel(hid_ref, gain_ref, rope_ref, pos_ref, wk_ref, wv_ref, wq_ref,
                 q_ref, cos_ref, sin_ref, v_ref, own_ref, kall_ref, vall_ref, pall_ref,
                 hid_s, x_s, w_s, k_s, vt_s, hid_sem, w_sem, out_sem, send_sem, recv_sem):
    rows, width = hid_s.shape
    half = rows // 2
    mine = lax.axis_index("tp")
    me = lax.axis_index("cp")
    core = me + 1 - 2 * lax.rem(me, 2)
    far = lax.rem(me + 2, 4)
    nk = wk_ref.shape[1] // STEP
    nq = wq_ref.shape[1] // STEP
    first_q = 2 * nk
    part = rows // 4

    loads = [pltpu.make_async_copy(hid_ref.at[pl.ds(c * part, part), :], hid_s.at[pl.ds(c * part, part), :], hid_sem.at[c]) for c in range(4)]
    loads[0].start()
    loads[1].start()

    def weight(b):
        if b < first_q:
            w = wk_ref if b < nk else wv_ref
            return pltpu.make_async_copy(w.at[:, pl.ds((b % nk) * STEP, STEP)], w_s.at[b % SLOTS], w_sem.at[b % SLOTS])
        return q_weight(b - first_q)

    def q_weight(i):
        slot = lax.rem(i + first_q, SLOTS)
        return pltpu.make_async_copy(wq_ref.at[:, pl.ds(pl.multiple_of(i * STEP, STEP), STEP)], w_s.at[slot], w_sem.at[slot])

    barrier = pltpu.get_barrier_semaphore()
    for other in (core, far):
        pl.semaphore_signal(barrier, inc=1, device_id={"cp": other}, device_id_type=MESH)
    pl.semaphore_wait(barrier, 2)

    def send(n, src, dst, other):
        return pltpu.make_async_remote_copy(src_ref=src, dst_ref=dst, send_sem=send_sem.at[n], recv_sem=recv_sem.at[n], device_id={"cp": other}, device_id_type=MESH)

    far_p, core_p = send(0, pos_ref, pall_ref.at[2], far), send(1, pos_ref, pall_ref.at[1], core)
    relay_p = send(2, pall_ref.at[2], pall_ref.at[3], core)
    to_far, to_core, relay = [], [], []
    for b in range(first_q):
        cut = pl.ds((b % nk) * STEP, STEP)
        at = (slice(None), cut) if b < nk else (cut, slice(None))
        src, dst = (k_s, kall_ref) if b < nk else (vt_s, vall_ref)
        to_far.append(send(3 + 3 * b, src.at[at], dst.at[(2, *at)], far))
        to_core.append(send(4 + 3 * b, src.at[at], dst.at[(1, *at)], core))
        relay.append(send(5 + 3 * b, dst.at[(2, *at)], dst.at[(3, *at)], core))
    keep_p = pltpu.make_async_copy(pos_ref, pall_ref.at[0], out_sem.at[0])
    keep_k = pltpu.make_async_copy(k_s, kall_ref.at[0], out_sem.at[1])
    keep_v = pltpu.make_async_copy(vt_s, vall_ref.at[0], out_sem.at[2])
    keep_x = pltpu.make_async_copy(x_s.at[pl.ds(pl.multiple_of(mine * half, half), half), :], own_ref, out_sem.at[3])
    far_p.start()
    core_p.start()
    keep_p.start()
    for c in range(4):
        angle = jnp.broadcast_to(pos_ref[c:c + 1, :], (HEAD, HEAD)).T.astype(jnp.float32) * rope_ref[0:1, :]
        cos_ref[c * HEAD:(c + 1) * HEAD, :] = jnp.cos(angle)
        sin_ref[c * HEAD:(c + 1) * HEAD, :] = jnp.sin(angle) * rope_ref[1:2, :]

    group = 64
    for c in range(4):
        loads[c].wait()
        if c < 2:
            loads[c + 2].start()
        for b in ((), (), (0, 1), (2,))[c]:
            weight(b).start()

        @pl.loop(0, part // group)
        def _(g, c=c):
            r = pl.ds(pl.multiple_of(c * part + g * group, group), group)
            total = jnp.zeros((group, HEAD), jnp.float32)
            for j in range(width // HEAD):
                x = hid_s[r, j * HEAD:(j + 1) * HEAD].astype(jnp.float32)
                total += x * x
            inv = lax.rsqrt(jnp.sum(total, axis=-1, keepdims=True) * (1.0 / width) + EPS)
            inv = jnp.broadcast_to(inv, (group, HEAD))
            for j in range(width // HEAD):
                cols = slice(j * HEAD, (j + 1) * HEAD)
                x_s[r, cols] = (hid_s[r, cols].astype(jnp.float32) * inv * gain_ref[:, cols]).astype(jnp.bfloat16)

    for b in range(first_q):
        weight(b).wait()
        weight(2 * b + 3).start()
        weight(2 * b + 4).start()

        @pl.loop(0, 2)
        def _(j, b=b):
            r = pl.ds(pl.multiple_of(j * half, half), half)
            out = dot(x_s[r, :], w_s[b % SLOTS]).astype(jnp.bfloat16)
            for h in range(STEP // HEAD):
                piece = out[:, h * HEAD:(h + 1) * HEAD]
                cols = pl.ds((b % nk) * STEP + h * HEAD, HEAD)
                if b < nk:
                    k_s[r, cols] = rotate(piece.astype(jnp.float32), cos_ref[r, :], sin_ref[r, :])
                else:
                    v_ref[r, cols] = piece
                    vt_s[cols, r] = piece.T

        to_far[b].start()
        to_core[b].start()
        if b == nk - 1:
            keep_k.start()
    keep_v.start()

    @pl.loop(0, nq)
    def _(i):
        slot = lax.rem(i + first_q, SLOTS)
        q_weight(i).wait()

        @pl.when(i < nq - SLOTS + 1)
        def _():
            q_weight(i + SLOTS - 1).start()

        r = pl.ds(pl.multiple_of((1 - mine) * half, half), half)
        q_ref[:, pl.ds(pl.multiple_of(i * STEP, STEP), STEP)] = dot(x_s[r, :], w_s[slot]).astype(jnp.bfloat16)

        @pl.when(i == 1)
        def _():
            keep_x.start()

        for b, turn in enumerate((3, 6, 10, 14)):
            @pl.when(i == turn)
            def _(b=b):
                if b == 0:
                    far_p.wait_recv()
                    relay_p.start()
                to_far[b].wait_recv()
                relay[b].start()

    for copy in (keep_p, keep_k, keep_v, keep_x):
        copy.wait()
    for copy in (far_p, *to_far):
        copy.wait_send()
    for copy in (core_p, relay_p, *to_core, *relay):
        copy.wait()


def front(hidden, gain, rope, pos, w_key, w_value, w_query):
    rows, width = hidden.shape
    half, kvw, qw = rows // 2, w_key.shape[1], w_query.shape[1]
    bf16 = jnp.bfloat16
    return pl.pallas_call(
        front_kernel,
        out_shape=(
            jax.ShapeDtypeStruct((half, qw), bf16),
            jax.ShapeDtypeStruct((rows, HEAD), jnp.float32),
            jax.ShapeDtypeStruct((rows, HEAD), jnp.float32),
            jax.ShapeDtypeStruct((rows, kvw), bf16),
            jax.ShapeDtypeStruct((half, width), bf16),
            jax.ShapeDtypeStruct((4, rows, kvw), bf16),
            jax.ShapeDtypeStruct((4, kvw, rows), bf16),
            jax.ShapeDtypeStruct((4, *pos.shape), jnp.int32),
        ),
        in_specs=[ANY, VMEM, VMEM, VMEM, ANY, ANY, ANY],
        out_specs=(VMEM, VMEM, VMEM, VMEM, ANY, ANY, ANY, ANY),
        scratch_shapes=[
            pltpu.VMEM((rows, width), bf16),
            pltpu.VMEM((rows, width), bf16),
            pltpu.VMEM((SLOTS, width, STEP), bf16),
            pltpu.VMEM((rows, kvw), bf16),
            pltpu.VMEM((kvw, rows), bf16),
            pltpu.SemaphoreType.DMA((4,)),
            pltpu.SemaphoreType.DMA((SLOTS,)),
            pltpu.SemaphoreType.DMA((4,)),
            pltpu.SemaphoreType.DMA((3 + 6 * kvw // STEP,)),
            pltpu.SemaphoreType.DMA((3 + 6 * kvw // STEP,)),
        ],
        compiler_params=pltpu.CompilerParams(collective_id=0, has_side_effects=True, vmem_limit_bytes=62 * 1024 * 1024),
        cost_estimate=pl.CostEstimate(flops=2 * rows * width * (2 * kvw + qw // 2), bytes_accessed=2 * width * (rows + 2 * kvw + qw), transcendentals=0),
    )(hidden, gain, rope, pos, w_key, w_value, w_query)


def attn_kernel(lead, row_ref, q_ref, cos_ref, sin_ref, qpos_ref, kpos_ref, k_ref, vt_ref, token_ref, *rest):
    if lead:
        w_ref, o_ref, part_ref, kp_s, q_s, s_s, m_s, l_s, acc_s, min_s, w_s, ctx_s, w_sem = rest
        load = pltpu.make_async_copy(w_ref.at[:, 0:lead], w_s, w_sem)
    else:
        o_ref, kp_s, q_s, s_s, m_s, l_s, acc_s, min_s = rest
    blocks, rows = k_ref.shape[0], k_ref.shape[1]
    groups, wide = acc_s.shape[0], acc_s.shape[2]
    pair = wide // Q_ROWS
    qpos = qpos_ref[...].reshape(1, Q_ROWS)

    @pl.when(pl.program_id(0) == 0)
    def _():
        if lead:
            load.start()
        span = rows // HEAD
        for b in range(blocks):
            for n in range(span):
                kp_s[b, n * HEAD:(n + 1) * HEAD, :] = jnp.broadcast_to(kpos_ref[b * span + n:b * span + n + 1, :], (HEAD, HEAD)).T
            min_s[b] = jnp.min(kpos_ref[b * span:(b + 1) * span, :])

    min_s[blocks] = jnp.max(qpos)
    for g in range(groups * pair):
        x = q_ref[:, g * HEAD:(g + 1) * HEAD].astype(jnp.float32)
        q_s[g // pair, (g % pair) * Q_ROWS:(g % pair + 1) * Q_ROWS, :] = rotate(x, cos_ref[...], sin_ref[...])
    m_s[...] = jnp.full_like(m_s, NEG_BIG)
    l_s[...] = jnp.zeros_like(l_s)
    acc_s[...] = jnp.zeros_like(acc_s)

    @pl.loop(0, blocks)
    def _(b):
        @pl.when(min_s[b] <= min_s[blocks])
        def _():
            k = k_ref[b]
            allowed = jnp.concatenate([kp_s[b] <= qpos] * pair, axis=1)
            for g in range(groups):
                s = lax.dot_general(k, q_s[g], (((1,), (1,)), ((), ())), preferred_element_type=jnp.float32)
                s = jnp.where(allowed, s, NEG_BIG)
                s_s[b, g] = s
                m_s[g] = jnp.maximum(m_s[g], jnp.max(s.reshape(rows // 8, 8, wide), axis=0))

    for g in range(groups):
        m_s[g] = jnp.broadcast_to(jnp.max(m_s[g], axis=0, keepdims=True), (8, wide)) * EXP_SCALE

    @pl.loop(0, blocks)
    def _(b):
        @pl.when(min_s[b] <= min_s[blocks])
        def _():
            vt = vt_ref[b]
            for g in range(groups):
                p = jnp.exp2(s_s[b, g].reshape(rows // 8, 8, wide) * EXP_SCALE - m_s[g][None])
                l_s[g] += jnp.sum(p, axis=0)
                acc_s[g] += dot(vt, p.reshape(rows, wide).astype(jnp.bfloat16))

    for g in range(groups * pair):
        cols = slice((g % pair) * Q_ROWS, (g % pair + 1) * Q_ROWS)
        o = acc_s[g // pair, :, cols] / jnp.sum(l_s[g // pair, :, cols], axis=0, keepdims=True)
        o_ref[:, g * HEAD:(g + 1) * HEAD] = o.T.astype(jnp.bfloat16)

    if lead:
        ctx_s[pl.program_id(0)] = o_ref[...]

        @pl.when(pl.program_id(0) == pl.num_programs(0) - 1)
        def _():
            load.wait()
            ctx = jnp.concatenate([ctx_s[n] for n in range(ctx_s.shape[0])], axis=1)
            part_ref[...] = dot(ctx, w_s[...])


def attention(q, r, count, cos, sin, pos, k_all, vt_all, kpos, block, token, w_out=None, lead=0):
    blocks, brows, kvw = k_all.shape
    width = q.shape[1]
    rows = count * Q_ROWS
    per = q.shape[0] // Q_ROWS
    kv = kvw // HEAD
    g = width // kvw
    wide = PAIR * Q_ROWS
    table = pl.BlockSpec((Q_ROWS, HEAD), lambda n, s: (s[0] * per + r + lax.div(n, kv), 0))
    unit = lambda first: pl.BlockSpec((Q_ROWS, g * HEAD), lambda n, s: (first + lax.div(n, kv), lax.rem(n, kv)))
    return pl.pallas_call(
        functools.partial(attn_kernel, lead),
        out_shape=(jax.ShapeDtypeStruct((rows, width), jnp.bfloat16), *([jax.ShapeDtypeStruct((rows, lead), jnp.float32)] if lead else [])),
        grid_spec=pltpu.PrefetchScalarGridSpec(
            num_scalar_prefetch=1,
            grid=(count * kv,),
            in_specs=[
                unit(r),
                table,
                table,
                pl.BlockSpec((None, 1, HEAD), lambda n, s: (s[0] * per + r + lax.div(n, kv), 0, 0)),
                pl.BlockSpec(kpos.shape, lambda n, s: (0, 0)),
                pl.BlockSpec((blocks, brows, HEAD), lambda n, s: (0, 0, lax.rem(n, kv))),
                pl.BlockSpec((blocks, HEAD, brows), lambda n, s: (0, lax.rem(n, kv), 0)),
                ANY,
                *([ANY] if lead else []),
            ],
            out_specs=(unit(0), *([pl.BlockSpec((rows, lead), lambda n, s: (0, 0))] if lead else [])),
            scratch_shapes=[
                pltpu.VMEM((blocks, brows, HEAD), jnp.int32),
                pltpu.VMEM((g // PAIR, wide, HEAD), jnp.bfloat16),
                pltpu.VMEM((blocks, g // PAIR, brows, wide), jnp.float32),
                pltpu.VMEM((g // PAIR, 8, wide), jnp.float32),
                pltpu.VMEM((g // PAIR, 8, wide), jnp.float32),
                pltpu.VMEM((g // PAIR, HEAD, wide), jnp.float32),
                pltpu.SMEM((blocks + 1,), jnp.int32),
                *([pltpu.VMEM((width, lead), jnp.bfloat16), pltpu.VMEM((kv, Q_ROWS, g * HEAD), jnp.bfloat16), pltpu.SemaphoreType.DMA] if lead else []),
            ],
        ),
        cost_estimate=pl.CostEstimate(flops=4 * rows * width * blocks * brows, bytes_accessed=rows * width * 4, transcendentals=rows * blocks * brows * kv * g),
    )(block, q, cos, sin, pos[:, None, :], kpos, k_all, vt_all, token, *([w_out] if lead else []))


def q_kernel(x_ref, w_ref, token_ref, o_ref):
    o_ref[...] = dot(x_ref[...], w_ref[...]).astype(jnp.bfloat16)


def project_q(x, w, token, step=512):
    rows = x.shape[0]
    depth, width = w.shape
    return pl.pallas_call(
        q_kernel,
        out_shape=jax.ShapeDtypeStruct((rows, width), jnp.bfloat16),
        grid=(width // step,),
        in_specs=[pl.BlockSpec((rows, depth), lambda n: (0, 0)), pl.BlockSpec((depth, step), lambda n: (0, n)), ANY],
        out_specs=pl.BlockSpec((rows, step), lambda n: (0, n)),
        cost_estimate=pl.CostEstimate(flops=2 * rows * depth * width, bytes_accessed=2 * (rows + width) * depth, transcendentals=0),
    )(x, w, token)


def part_kernel(x_ref, w_ref, token_ref, o_ref):
    o_ref[...] = dot(x_ref[...], w_ref[...])


def project_out(x, w, start, cols, token, step=512):
    rows, depth = x.shape
    return pl.pallas_call(
        part_kernel,
        out_shape=jax.ShapeDtypeStruct((rows, cols), jnp.float32),
        grid=(cols // step,),
        in_specs=[pl.BlockSpec((rows, depth), lambda n: (0, 0)), pl.BlockSpec((depth, step), lambda n: (0, start // step + n)), ANY],
        out_specs=pl.BlockSpec((rows, step), lambda n: (0, n)),
        cost_estimate=pl.CostEstimate(flops=2 * rows * depth * cols, bytes_accessed=2 * (rows + cols) * depth, transcendentals=0),
    )(x, w, token)


def final_kernel(row_ref, x_ref, w_ref, hid_ref, pa_ref, pb_ref, *rest):
    final_ref, o_ref = rest[-2:]
    top = pa_ref.shape[0]
    mine = dot(x_ref[...], w_ref[...])
    for p_ref, r in ((pa_ref, slice(0, top)), (pb_ref, slice(top, 2 * top))):
        total = mine[r] + p_ref[...]
        final = (hid_ref[r, :].astype(jnp.float32) + total).astype(jnp.bfloat16)
        final_ref[r, :] = final
        o_ref[r, :] = final


def finish(x, w, hidden, row, parts, start, cols, out, step=512):
    rows, depth = x.shape
    part = rows // 2
    first = start // step
    block = pl.BlockSpec((rows, step), lambda n, r: (r[0], first + n))
    return pl.pallas_call(
        final_kernel,
        out_shape=(jax.ShapeDtypeStruct((rows, cols), jnp.bfloat16), jax.ShapeDtypeStruct(hidden.shape, jnp.bfloat16)),
        grid_spec=pltpu.PrefetchScalarGridSpec(
            num_scalar_prefetch=1,
            grid=(cols // step,),
            in_specs=[
                pl.BlockSpec((rows, depth), lambda n, r: (0, 0)),
                pl.BlockSpec((depth, step), lambda n, r: (0, first + n)),
                block,
                pl.BlockSpec((part, step), lambda n, r: (0, n)),
                pl.BlockSpec((part, step), lambda n, r: (0, n)),
                *([] if out is None else [ANY]),
            ],
            out_specs=(pl.BlockSpec((rows, step), lambda n, r: (0, n)), block),
        ),
        input_output_aliases={} if out is None else {6: 1},
        cost_estimate=pl.CostEstimate(flops=2 * rows * depth * cols, bytes_accessed=2 * (rows + cols) * depth, transcendentals=0),
    )(row, x, w, hidden, *parts, *([] if out is None else [out]))


def place_kernel(row_ref, *refs):
    xs, o_ref = refs[:-2], refs[-1]
    start = 0
    for x_ref in xs:
        o_ref[:, start:start + x_ref.shape[1]] = x_ref[...]
        start += x_ref.shape[1]


def place(out, pieces, row, start):
    rows = pieces[0].shape[0]
    cols = sum(x.shape[1] for x in pieces)
    step = 64 if cols > 1024 else rows
    per = rows // step
    return pl.pallas_call(
        place_kernel,
        out_shape=jax.ShapeDtypeStruct(out.shape, out.dtype),
        grid_spec=pltpu.PrefetchScalarGridSpec(
            num_scalar_prefetch=1,
            grid=(per,),
            in_specs=[*(pl.BlockSpec((step, x.shape[1]), lambda n, r: (n, 0)) for x in pieces), ANY],
            out_specs=pl.BlockSpec((step, cols), lambda n, r: (r[0] * per + n, start // cols)),
        ),
        input_output_aliases={1 + len(pieces): 0},
        cost_estimate=pl.CostEstimate(flops=0, bytes_accessed=4 * rows * cols, transcendentals=0),
    )(row, *pieces, out)


def solution(mesh):
    swap_tp = [(0, 1), (1, 0)]

    def then_send(kernel, *args):
        got = kernel(*args)
        out = got[0] if kernel is finish else got[1] if kernel is attention else got
        return got, lax.ppermute(out, "tp", swap_tp)

    def local_block(hidden, tok_pos, norm_gain, w_query, w_key, w_value, w_out):
        rows, _ = hidden.shape
        half = rows // 2
        kv = w_key.shape[1] // HEAD
        t = lax.axis_index("tp").astype(jnp.int32)
        own, send = t[None], 1 - t[None]
        pos = tok_pos.reshape(-1, HEAD)
        q, cos, sin, v, own_x, k_all, vt_all, p_all = front(hidden, norm_gain[None, :], rope_rows(), pos, w_key, w_value, w_query)
        kpos = p_all.reshape(-1, HEAD)
        chunks = [(a, b - a) for a, b in zip(CUTS, CUTS[1:])]
        token = q
        parts = []
        for r in range(half // Q_ROWS):
            (ctx, token), part = then_send(attention, q, r, 1, cos, sin, pos, k_all, vt_all, kpos, send, token, w_out, CUTS[1])
            parts.append([part])
            for start, cols in chunks[1:]:
                token, part = then_send(project_out, ctx, w_out, start, cols, token)
                parts[r].append(part)
        q = project_q(own_x, w_query, token)
        ctx = attention(q, 0, half // Q_ROWS, cos, sin, pos, k_all, vt_all, kpos, own, q)[0]
        out = None
        others = []
        for c, (start, cols) in enumerate(chunks):
            (_, out), other = then_send(finish, ctx, w_out, hidden, own, [p[c] for p in parts], start, cols, out)
            others.append(other)
        out = place(out, others[:-1], send, 0)
        out = place(out, others[-1:], send, CUTS[-2])
        return out, k_all[0].reshape(rows, kv, HEAD), v.reshape(rows, kv, HEAD)

    row_spec = P(("dp", "cp"), None)
    cache_spec = P(("dp", "cp"), "tp", None)

    return jax.shard_map(local_block, mesh=mesh, in_specs=(row_spec, P(("dp", "cp")), P(None), P(None, "tp"), P(None, "tp"), P(None, "tp"), P("tp", None)), out_specs=(row_spec, cache_spec, cache_spec), check_vma=False)
```

profile of v0, /device:TPU:2, one launch (start us, length us, event | category | flops | bytes accessed | tf_op | source)
XLA Modules:
  0.0 365.2 jit_solution(4053574663991463014)
XLA Ops:
  0.7 0.6 pad_maximum_fusion.rope_ref
  1.2 40.0 %shard_map.94 = (bf16[256,4096]{1,0:T(8,128)(2,1)}, f32[512,128]{1,0:T(8,128)}, f32[512,128]{1,0:T(8,128)}, bf16[512,512]{1,0:T(8,128)(2,1)}, bf16[256,8192]{1,0...) custom-call(bf16[512,8192]{1,0:T(8,128)(2,1)} %hid_ref.11, ...), custom_call_target="tpu_custom_call" | custom-call | flops 25769803776 | bytes 92274688 | tf_op jit(solution)/shard_map/pallas_call | solution.py:180
  41.2 14.2 %shard_map.95 = (bf16[128,4096]{1,0:T(8,128)(2,1)}, f32[128,1024]{1,0:T(8,128)}) custom-call(s32[1]{0:T(128)S(6)} %sub.3.row_ref, bf16[256,4096]{1,0:T(8,128)(2,1)} %get-tuple-element.26.q_ref.token_ref, f32[512,128]{1,0:T(8,128)} %get-tuple-element.27.cos_ref, f32[512,128]{1,0:T(8,128)} %get-tuple-element.28.sin_ref, s32[4,1,128]{2,1,0:T(1,128)} %bitcast.9, ...), custom_call_target="tpu_custom_call" | custom-call | flops 4294967296 | bytes 2097152 | tf_op jit(solution)/shard_map/pallas_call | solution.py:290
  55.4 9.3 %collective-permute-start.8 = (f32[128,1024]{1,0:T(8,128)}, f32[128,1024]{1,0:T(8,128)}, u32[]{:S(2)}, u32[]{:S(2)}) collective-permute-start(f32[128,1024]{1,0:T(8,128)} %get-tuple-element.33.token_ref), channel_id=1, source_target_pairs={{0,4},{4,0},{1,5},{5,1},{2,6},{6,2},{3,7},{7,3}} | collective-permute-start | bytes 1572872 | tf_op jit(solution)/shard_map/ppermute | solution.py:426
  64.7 8.5 %shard_map.96.token_ref = f32[128,2048]{1,0:T(8,128)} custom-call(bf16[128,4096]{1,0:T(8,128)(2,1)} %get-tuple-element.32.x_ref, bf16[4096,8192]{1,0:T(8,128)(2,1)} %w_ref.27, f32[128,1024]{1,0:T(8,128)} %get-tuple-element.33.token_ref), custom_call_target="tpu_custom_call" | custom-call | flops 2147483648 | bytes 17825792 | tf_op jit(solution)/shard_map/pallas_call | solution.py:346
  73.2 0.0 collective-permute-start.6
  73.3 8.5 %shard_map.97.token_ref = f32[128,2048]{1,0:T(8,128)} custom-call(bf16[128,4096]{1,0:T(8,128)(2,1)} %get-tuple-element.32.x_ref, bf16[4096,8192]{1,0:T(8,128)(2,1)} %w_ref.27, f32[128,2048]{1,0:T(8,128)} %shard_map.96.token_ref), custom_call_target="tpu_custom_call" | custom-call | flops 2147483648 | bytes 17825792 | tf_op jit(solution)/shard_map/pallas_call | solution.py:346
  81.8 8.5 %shard_map.98.token_ref = f32[128,2048]{1,0:T(8,128)} custom-call(bf16[128,4096]{1,0:T(8,128)(2,1)} %get-tuple-element.32.x_ref, bf16[4096,8192]{1,0:T(8,128)(2,1)} %w_ref.27, f32[128,2048]{1,0:T(8,128)} %shard_map.97.token_ref), custom_call_target="tpu_custom_call" | custom-call | flops 2147483648 | bytes 17825792 | tf_op jit(solution)/shard_map/pallas_call | solution.py:346
  90.3 5.2 %shard_map.99.token_ref = f32[128,1024]{1,0:T(8,128)} custom-call(bf16[128,4096]{1,0:T(8,128)(2,1)} %get-tuple-element.32.x_ref, bf16[4096,8192]{1,0:T(8,128)(2,1)} %w_ref.27, f32[128,2048]{1,0:T(8,128)} %shard_map.98.token_ref), custom_call_target="tpu_custom_call" | custom-call | flops 1073741824 | bytes 9437184 | tf_op jit(solution)/shard_map/pallas_call | solution.py:346
  95.5 14.2 %shard_map.100 = (bf16[128,4096]{1,0:T(8,128)(2,1)}, f32[128,1024]{1,0:T(8,128)}) custom-call(s32[1]{0:T(128)S(6)} %sub.3.row_ref, bf16[256,4096]{1,0:T(8,128)(2,1)} %get-tuple-element.26.q_ref.token_ref, f32[512,128]{1,0:T(8,128)} %get-tuple-element.27.cos_ref, f32[512,128]{1,0:T(8,128)} %get-tuple-element.28.sin_ref, s32[4,1,128]{2,1,0:T(1,128)} %bitcast.10, ...), custom_call_target="tpu_custom_call" | custom-call | flops 4294967296 | bytes 2097152 | tf_op jit(solution)/shard_map/pallas_call | solution.py:290
  109.7 9.8 %collective-permute-start.9 = (f32[128,1024]{1,0:T(8,128)}, f32[128,1024]{1,0:T(8,128)}, u32[]{:S(2)}, u32[]{:S(2)}) collective-permute-start(f32[128,1024]{1,0:T(8,128)} %get-tuple-element.35.token_ref), channel_id=1, source_target_pairs={{0,4},{4,0},{1,5},{5,1},{2,6},{6,2},{3,7},{7,3}} | collective-permute-start | bytes 1572872 | tf_op jit(solution)/shard_map/ppermute | solution.py:426
  119.5 8.5 %shard_map.101.token_ref = f32[128,2048]{1,0:T(8,128)} custom-call(bf16[128,4096]{1,0:T(8,128)(2,1)} %get-tuple-element.34.x_ref, bf16[4096,8192]{1,0:T(8,128)(2,1)} %w_ref.27, f32[128,1024]{1,0:T(8,128)} %get-tuple-element.35.token_ref), custom_call_target="tpu_custom_call" | custom-call | flops 2147483648 | bytes 17825792 | tf_op jit(solution)/shard_map/pallas_call | solution.py:346
  128.0 0.0 collective-permute-start.7
  128.1 8.5 %shard_map.102.token_ref = f32[128,2048]{1,0:T(8,128)} custom-call(bf16[128,4096]{1,0:T(8,128)(2,1)} %get-tuple-element.34.x_ref, bf16[4096,8192]{1,0:T(8,128)(2,1)} %w_ref.27, f32[128,2048]{1,0:T(8,128)} %shard_map.101.token_ref), custom_call_target="tpu_custom_call" | custom-call | flops 2147483648 | bytes 17825792 | tf_op jit(solution)/shard_map/pallas_call | solution.py:346
  136.6 8.5 %shard_map.103.token_ref = f32[128,2048]{1,0:T(8,128)} custom-call(bf16[128,4096]{1,0:T(8,128)(2,1)} %get-tuple-element.34.x_ref, bf16[4096,8192]{1,0:T(8,128)(2,1)} %w_ref.27, f32[128,2048]{1,0:T(8,128)} %shard_map.102.token_ref), custom_call_target="tpu_custom_call" | custom-call | flops 2147483648 | bytes 17825792 | tf_op jit(solution)/shard_map/pallas_call | solution.py:346
  145.0 2.0 collective-permute-start.3
  147.0 5.2 %shard_map.104.token_ref = f32[128,1024]{1,0:T(8,128)} custom-call(bf16[128,4096]{1,0:T(8,128)(2,1)} %get-tuple-element.34.x_ref, bf16[4096,8192]{1,0:T(8,128)(2,1)} %w_ref.27, f32[128,2048]{1,0:T(8,128)} %shard_map.103.token_ref), custom_call_target="tpu_custom_call" | custom-call | flops 1073741824 | bytes 9437184 | tf_op jit(solution)/shard_map/pallas_call | solution.py:346
  152.3 28.4 %shard_map.105.q_ref.token_ref = bf16[256,4096]{1,0:T(8,128)(2,1)} custom-call(bf16[256,8192]{1,0:T(8,128)(2,1)} %get-tuple-element.25.x_ref, bf16[8192,4096]{1,0:T(8,128)(2,1)} %w_ref.22, f32[128,1024]{1,0:T(8,128)} %shard_map.104.token_ref), custom_call_target="tpu_custom_call" | custom-call | flops 17179869184 | bytes 71303168 | tf_op jit(solution)/shard_map/pallas_call | solution.py:330
  180.7 0.0 collective-permute-done.8.pa_ref
  180.7 0.1 collective-permute-start.5
  180.7 2.0 collective-permute-start.2
  182.7 0.0 collective-permute-start.4
  182.8 38.3 %shard_map.106.x_ref = bf16[256,4096]{1,0:T(8,128)(2,1)} custom-call(s32[1]{0:T(128)} %bitcast.row_ref, bf16[256,4096]{1,0:T(8,128)(2,1)} %shard_map.105.q_ref.token_ref, f32[512,128]{1,0:T(8,128)} %get-tuple-element.27.cos_ref, f32[512,128]{1,0:T(8,128)} %get-tuple-element.28.sin_ref, s32[4,1,128]{2,1,0:T(1,128)} %bitcast.11, s32[16,128]{1,0:T(8,128)} %bitcast.7, ...), custom_call_target="tpu_custom_call" | custom-call | flops 8589934592 | bytes 4194304 | tf_op jit(solution)/shard_map/pallas_call | solution.py:290
  221.1 6.6 %shard_map.107 = (bf16[256,1024]{1,0:T(8,128)(2,1)}, bf16[512,8192]{1,0:T(8,128)(2,1)}) custom-call(s32[1]{0:T(128)} %bitcast.row_ref, bf16[256,4096]{1,0:T(8,128)(2,1)} %shard_map.106.x_ref, bf16[4096,8192]{1,0:T(8,128)(2,1)} %w_ref.27, bf16[512,8192]{1,0:T(8,128)(2,1)} %hid_ref.11, f32[128,1024]{1,0:T(8,128)} %collective-permute-done.8.pa_ref, ...), custom_call_target="tpu_custom_call" | custom-call | flops 2147483648 | bytes 10485760 | tf_op jit(solution)/shard_map/pallas_call | solution.py:372
  227.6 0.0 collective-permute-done.6.pa_ref
  227.6 0.0 collective-permute-start
  227.7 11.0 %shard_map.108 = (bf16[256,2048]{1,0:T(8,128)(2,1)}, bf16[512,8192]{1,0:T(8,128)(2,1)}) custom-call(s32[1]{0:T(128)} %bitcast.row_ref, bf16[256,4096]{1,0:T(8,128)(2,1)} %shard_map.106.x_ref, bf16[4096,8192]{1,0:T(8,128)(2,1)} %w_ref.27, bf16[512,8192]{1,0:T(8,128)(2,1)} %hid_ref.11, ...), custom_call_target="tpu_custom_call", output_to_operand_aliasing={{1}: (6, {})} | custom-call | flops 4294967296 | bytes 18874368 | tf_op jit(solution)/shard_map/pallas_call | solution.py:372
  238.7 2.0 collective-permute-start.1
  240.7 11.1 %collective-permute-done.4.pa_ref = f32[128,2048]{1,0:T(8,128)} collective-permute-done((f32[128,2048]{1,0:T(8,128)S(1)}, f32[128,2048]{1,0:T(8,128)}, u32[]{:S(2)}, u32[]{:S(2)}) %collective-permute-start.4) | collective-permute-done | bytes 1048608 | tf_op jit(solution)/shard_map/ppermute | solution.py:426
  251.8 10.9 %shard_map.109 = (bf16[256,2048]{1,0:T(8,128)(2,1)}, bf16[512,8192]{1,0:T(8,128)(2,1)}) custom-call(s32[1]{0:T(128)} %bitcast.row_ref, bf16[256,4096]{1,0:T(8,128)(2,1)} %shard_map.106.x_ref, bf16[4096,8192]{1,0:T(8,128)(2,1)} %w_ref.27, bf16[512,8192]{1,0:T(8,128)(2,1)} %hid_ref.11, ...), custom_call_target="tpu_custom_call", output_to_operand_aliasing={{1}: (6, {})} | custom-call | flops 4294967296 | bytes 18874368 | tf_op jit(solution)/shard_map/pallas_call | solution.py:372
  262.7 11.0 %shard_map.110 = (bf16[256,2048]{1,0:T(8,128)(2,1)}, bf16[512,8192]{1,0:T(8,128)(2,1)}) custom-call(s32[1]{0:T(128)} %bitcast.row_ref, bf16[256,4096]{1,0:T(8,128)(2,1)} %shard_map.106.x_ref, bf16[4096,8192]{1,0:T(8,128)(2,1)} %w_ref.27, bf16[512,8192]{1,0:T(8,128)(2,1)} %hid_ref.11, ...), custom_call_target="tpu_custom_call", output_to_operand_aliasing={{1}: (6, {})} | custom-call | flops 4294967296 | bytes 18874368 | tf_op jit(solution)/shard_map/pallas_call | solution.py:372
  273.7 0.0 collective-permute-start.14
  273.7 2.0 collective-permute-start.13
  275.7 0.0 collective-permute-start.12
  275.8 2.0 collective-permute-start.11
  277.8 0.8 copy-done.5
  278.6 6.6 %shard_map.111 = (bf16[256,1024]{1,0:T(8,128)(2,1)}, bf16[512,8192]{1,0:T(8,128)(2,1)}) custom-call(s32[1]{0:T(128)} %bitcast.row_ref, bf16[256,4096]{1,0:T(8,128)(2,1)} %shard_map.106.x_ref, bf16[4096,8192]{1,0:T(8,128)(2,1)} %w_ref.27, bf16[512,8192]{1,0:T(8,128)(2,1)} %hid_ref.11, ...), custom_call_target="tpu_custom_call", output_to_operand_aliasing={{1}: (6, {})} | custom-call | flops 2147483648 | bytes 10485760 | tf_op jit(solution)/shard_map/pallas_call | solution.py:372
  285.1 0.0 collective-permute-start.10
  285.2 1.1 slice.3
  286.3 2.0 reshape.64
  288.2 0.9 reshape_squeeze.3
  289.1 67.1 %collective-permute-done.11.refs_0_ = bf16[256,1024]{1,0:T(8,128)(2,1)} collective-permute-done((bf16[256,1024]{1,0:T(8,128)(2,1)}, bf16[256,1024]{1,0:T(8,128)(2,1)}, u32[]{:S(2)}, u32[]{:S(2)}) %collective-permute-start.11) | collective-permute-done | bytes 524320 | tf_op jit(solution)/shard_map/ppermute | solution.py:426
  356.3 1.0 copy-done.3
  357.2 0.4 copy-done.4
  357.6 4.4 %shard_map.112.refs_1_ = bf16[512,8192]{1,0:T(8,128)(2,1)} custom-call(s32[1]{0:T(128)S(6)} %sub.3.row_ref, bf16[256,1024]{1,0:T(8,128)(2,1)} %collective-permute-done.11.refs_0_, bf16[256,2048]{1,0:T(8,128)(2,1)} %collective-permute-done.12.refs_1_, bf16[256,2048]{1,0:T(8,128)(2,1)} %copy-done.4, ...), custom_call_target="tpu_custom_call", output_to_operand_aliasing={{}: (5, {})} | custom-call | bytes 7340032 | tf_op jit(solution)/shard_map/pallas_call | solution.py:406
  362.0 0.5 collective-permute-done.10.refs_0_
  362.5 0.8 copy-done.6
  363.3 1.9 shard_map.113
  (21 shorter events, 0.1 us)
Async XLA Ops:
  55.4 125.2 %collective-permute-start.8 = (f32[128,1024]{1,0:T(8,128)}, f32[128,1024]{1,0:T(8,128)}, u32[]{:S(2)}, u32[]{:S(2)}) collective-permute-start(f32[128,1024]{1,0:T(8,128)} %get-tuple-element.33.token_ref), channel_id=1, source_target_pairs={{0,4},{4,0},{1,5},{5,1},{2,6},{6,2},{3,7},{7,3}} | collective-permute-start | bytes 1572872 | tf_op jit(solution)/shard_map/ppermute | solution.py:426
  73.2 154.4 %collective-permute-start.6 = (f32[128,2048]{1,0:T(8,128)}, f32[128,2048]{1,0:T(8,128)}, u32[]{:S(2)}, u32[]{:S(2)}) collective-permute-start(f32[128,2048]{1,0:T(8,128)} %shard_map.96.token_ref), channel_id=1, source_target_pairs={{0,4},{4,0},{1,5},{5,1},{2,6},{6,2},{3,7},{7,3}} | collective-permute-start | bytes 3145736 | tf_op jit(solution)/shard_map/ppermute | solution.py:426
  109.7 71.0 %collective-permute-start.9 = (f32[128,1024]{1,0:T(8,128)}, f32[128,1024]{1,0:T(8,128)}, u32[]{:S(2)}, u32[]{:S(2)}) collective-permute-start(f32[128,1024]{1,0:T(8,128)} %get-tuple-element.35.token_ref), channel_id=1, source_target_pairs={{0,4},{4,0},{1,5},{5,1},{2,6},{6,2},{3,7},{7,3}} | collective-permute-start | bytes 1572872 | tf_op jit(solution)/shard_map/ppermute | solution.py:426
  128.0 54.7 %collective-permute-start.7 = (f32[128,2048]{1,0:T(8,128)}, f32[128,2048]{1,0:T(8,128)}, u32[]{:S(2)}, u32[]{:S(2)}) collective-permute-start(f32[128,2048]{1,0:T(8,128)} %shard_map.101.token_ref), channel_id=1, source_target_pairs={{0,4},{4,0},{1,5},{5,1},{2,6},{6,2},{3,7},{7,3}} | collective-permute-start | bytes 3145736 | tf_op jit(solution)/shard_map/ppermute | solution.py:426
  145.0 117.7 %collective-permute-start.3 = (f32[128,2048]{1,0:T(8,128)}, f32[128,2048]{1,0:T(8,128)}, u32[]{:S(2)}, u32[]{:S(2)}) collective-permute-start(f32[128,2048]{1,0:T(8,128)} %shard_map.103.token_ref), channel_id=1, source_target_pairs={{0,4},{4,0},{1,5},{5,1},{2,6},{6,2},{3,7},{7,3}} | collective-permute-start | bytes 3145736 | tf_op jit(solution)/shard_map/ppermute | solution.py:426
  152.3 28.4 %copy-start.2 = (f32[128,2048]{1,0:T(8,128)S(1)}, f32[128,2048]{1,0:T(8,128)}, u32[]{:S(2)}) copy-start(f32[128,2048]{1,0:T(8,128)} %shard_map.102.token_ref) | copy-start | bytes 3145732
  152.3 28.5 %copy-start = (f32[128,2048]{1,0:T(8,128)S(1)}, f32[128,2048]{1,0:T(8,128)}, u32[]{:S(2)}) copy-start(f32[128,2048]{1,0:T(8,128)} %shard_map.98.token_ref) | copy-start | bytes 3145732
  152.3 30.4 %copy-start.1 = (f32[128,2048]{1,0:T(8,128)S(1)}, f32[128,2048]{1,0:T(8,128)}, u32[]{:S(2)}) copy-start(f32[128,2048]{1,0:T(8,128)} %shard_map.97.token_ref) | copy-start | bytes 3145732
  180.7 58.0 %collective-permute-start.5 = (f32[128,2048]{1,0:T(8,128)S(1)}, f32[128,2048]{1,0:T(8,128)}, u32[]{:S(2)}, u32[]{:S(2)}) collective-permute-start(f32[128,2048]{1,0:T(8,128)S(1)} %copy-done.2), channel_id=1, source_target_pairs={{0,4},{4,0},{1,5},{5,1},{2,6},{6,2},{3,7},{7,3}} | collective-permute-start | bytes 3145736 | tf_op jit(solution)/shard_map/ppermute | solution.py:426
  180.7 82.0 %collective-permute-start.2 = (f32[128,2048]{1,0:T(8,128)S(1)}, f32[128,2048]{1,0:T(8,128)}, u32[]{:S(2)}, u32[]{:S(2)}) collective-permute-start(f32[128,2048]{1,0:T(8,128)S(1)} %copy-done), channel_id=1, source_target_pairs={{0,4},{4,0},{1,5},{5,1},{2,6},{6,2},{3,7},{7,3}} | collective-permute-start | bytes 3145736 | tf_op jit(solution)/shard_map/ppermute | solution.py:426
  182.7 69.0 %collective-permute-start.4 = (f32[128,2048]{1,0:T(8,128)S(1)}, f32[128,2048]{1,0:T(8,128)}, u32[]{:S(2)}, u32[]{:S(2)}) collective-permute-start(f32[128,2048]{1,0:T(8,128)S(1)} %copy-done.1), channel_id=1, source_target_pairs={{0,4},{4,0},{1,5},{5,1},{2,6},{6,2},{3,7},{7,3}} | collective-permute-start | bytes 3145736 | tf_op jit(solution)/shard_map/ppermute | solution.py:426
  227.6 48.1 %collective-permute-start = (f32[128,1024]{1,0:T(8,128)}, f32[128,1024]{1,0:T(8,128)}, u32[]{:S(2)}, u32[]{:S(2)}) collective-permute-start(f32[128,1024]{1,0:T(8,128)} %shard_map.99.token_ref), channel_id=1, source_target_pairs={{0,4},{4,0},{1,5},{5,1},{2,6},{6,2},{3,7},{7,3}} | collective-permute-start | bytes 1572872 | tf_op jit(solution)/shard_map/ppermute | solution.py:426
  238.7 39.1 %collective-permute-start.1 = (f32[128,1024]{1,0:T(8,128)}, f32[128,1024]{1,0:T(8,128)S(1)}, u32[]{:S(2)}, u32[]{:S(2)}) collective-permute-start(f32[128,1024]{1,0:T(8,128)} %shard_map.104.token_ref), channel_id=1, source_target_pairs={{0,4},{4,0},{1,5},{5,1},{2,6},{6,2},{3,7},{7,3}} | collective-permute-start | bytes 1572872 | tf_op jit(solution)/shard_map/ppermute | solution.py:426
  273.7 82.5 %collective-permute-start.14 = (bf16[256,2048]{1,0:T(8,128)(2,1)}, bf16[256,2048]{1,0:T(8,128)(2,1)S(1)}, u32[]{:S(2)}, u32[]{:S(2)}) collective-permute-start(bf16[256,2048]{1,0:T(8,128)(2,1)} %get-tuple-element.44), channel_id=1, source_target_pairs={{0,4},{4,0},{1,5},{5,1},{2,6},{6,2},{3,7},{7,3}} | collective-permute-start | bytes 3145736 | tf_op jit(solution)/shard_map/ppermute | solution.py:426
  273.7 82.5 %collective-permute-start.13 = (bf16[256,2048]{1,0:T(8,128)(2,1)}, bf16[256,2048]{1,0:T(8,128)(2,1)S(1)}, u32[]{:S(2)}, u32[]{:S(2)}) collective-permute-start(bf16[256,2048]{1,0:T(8,128)(2,1)} %get-tuple-element.43), channel_id=1, source_target_pairs={{0,4},{4,0},{1,5},{5,1},{2,6},{6,2},{3,7},{7,3}} | collective-permute-start | bytes 3145736 | tf_op jit(solution)/shard_map/ppermute | solution.py:426
  275.7 80.5 %collective-permute-start.12 = (bf16[256,2048]{1,0:T(8,128)(2,1)}, bf16[256,2048]{1,0:T(8,128)(2,1)}, u32[]{:S(2)}, u32[]{:S(2)}) collective-permute-start(bf16[256,2048]{1,0:T(8,128)(2,1)} %get-tuple-element.42), channel_id=1, source_target_pairs={{0,4},{4,0},{1,5},{5,1},{2,6},{6,2},{3,7},{7,3}} | collective-permute-start | bytes 3145736 | tf_op jit(solution)/shard_map/ppermute | solution.py:426
  275.8 80.4 %collective-permute-start.11 = (bf16[256,1024]{1,0:T(8,128)(2,1)}, bf16[256,1024]{1,0:T(8,128)(2,1)}, u32[]{:S(2)}, u32[]{:S(2)}) collective-permute-start(bf16[256,1024]{1,0:T(8,128)(2,1)} %get-tuple-element.41), channel_id=1, source_target_pairs={{0,4},{4,0},{1,5},{5,1},{2,6},{6,2},{3,7},{7,3}} | collective-permute-start | bytes 1572872 | tf_op jit(solution)/shard_map/ppermute | solution.py:426
  277.8 0.8 copy-start.5
  285.1 77.4 %collective-permute-start.10 = (bf16[256,1024]{1,0:T(8,128)(2,1)}, bf16[256,1024]{1,0:T(8,128)(2,1)S(1)}, u32[]{:S(2)}, u32[]{:S(2)}) collective-permute-start(bf16[256,1024]{1,0:T(8,128)(2,1)} %get-tuple-element.40), channel_id=1, source_target_pairs={{0,4},{4,0},{1,5},{5,1},{2,6},{6,2},{3,7},{7,3}} | collective-permute-start | bytes 1572872 | tf_op jit(solution)/shard_map/ppermute | solution.py:426
  356.2 1.0 copy-start.3
  356.2 1.3 copy-start.4
  362.5 0.8 copy-start.6
where the time goes:
time: 366 us; the launch traced here: 365 us
  Pallas kernels  249 us (68%)
  waiting for transfers between devices  78.7 us (22%)
  starting transfers between devices  29.4 us (8%)
  local copies, waits for them, and re-layouts  6.91 us (2%)
    ppermute x15, waiting for transfers between devices, then_send(): return (got, lax.ppermute(out, 'tp', swap_tp))  78.7 us
    pallas_call x3, Pallas kernels, attention(): pl.pallas_call(functools.partial(attn_kernel, lead), out_shape=(jax.Shape...  66.7 us
    pallas_call x8, Pallas kernels, project_out(): pl.pallas_call(part_kernel, out_shape=jax.ShapeDtypeStruct((rows, cols),...  61.4 us
    pallas_call x5, Pallas kernels, finish(): pl.pallas_call(final_kernel, out_shape=(jax.ShapeDtypeStruct((rows, cols)...  46.1 us
    pallas_call x1, Pallas kernels, front(): pl.pallas_call(front_kernel, out_shape=(jax.ShapeDtypeStruct((half, qw),...  40 us
    ppermute x15, starting transfers between devices, then_send(): return (got, lax.ppermute(out, 'tp', swap_tp))  29.4 us
    pallas_call x1, Pallas kernels, project_q(): pl.pallas_call(q_kernel, out_shape=jax.ShapeDtypeStruct((rows, width), jn...  28.4 us
  transfers between devices with their start and end apart: 15, of which 3 were waited for; matrix products, arithmetic and copies ran while one was open for 1% of the time, Pallas kernels for 53%

commit v1 on v0

--- a/solution.py
+++ b/solution.py
@@ -17,7 +17,7 @@
 PAIR = 2
 STEP = 256
 SLOTS = 8
-CUTS = (0, 1024, 3072, 5120, 7168, 8192)
+CUTS = (0, 1024, 3072, 5120, 7680, 8192)
 ANY = pl.BlockSpec(memory_space=pl.ANY)
 VMEM = pl.BlockSpec(memory_space=pltpu.VMEM)
 MESH = pl.DeviceIdType.MESH
@@ -38,7 +38,7 @@
 
 
 def front_kernel(hid_ref, gain_ref, rope_ref, pos_ref, wk_ref, wv_ref, wq_ref,
-                 q_ref, cos_ref, sin_ref, v_ref, own_ref, kall_ref, vall_ref, pall_ref,
+                 q_ref, cos_ref, sin_ref, v_ref, next_ref, own_ref, kall_ref, vall_ref, pall_ref,
                  hid_s, x_s, w_s, k_s, vt_s, hid_sem, w_sem, out_sem, send_sem, recv_sem):
     rows, width = hid_s.shape
     half = rows // 2
@@ -87,6 +87,7 @@
     keep_k = pltpu.make_async_copy(k_s, kall_ref.at[0], out_sem.at[1])
     keep_v = pltpu.make_async_copy(vt_s, vall_ref.at[0], out_sem.at[2])
     keep_x = pltpu.make_async_copy(x_s.at[pl.ds(pl.multiple_of(mine * half, half), half), :], own_ref, out_sem.at[3])
+    keep_next = pltpu.make_async_copy(x_s.at[pl.ds(pl.multiple_of((1 - mine) * half + part, part), part), :], next_ref, out_sem.at[4])
     far_p.start()
     core_p.start()
     keep_p.start()
@@ -149,14 +150,15 @@
         def _():
             q_weight(i + SLOTS - 1).start()
 
-        r = pl.ds(pl.multiple_of((1 - mine) * half, half), half)
+        r = pl.ds(pl.multiple_of((1 - mine) * half, half), part)
         q_ref[:, pl.ds(pl.multiple_of(i * STEP, STEP), STEP)] = dot(x_s[r, :], w_s[slot]).astype(jnp.bfloat16)
 
         @pl.when(i == 1)
         def _():
+            keep_next.start()
             keep_x.start()
 
-        for b, turn in enumerate((3, 6, 10, 14)):
+        for b, turn in enumerate((2, 5, 9, 13)):
             @pl.when(i == turn)
             def _(b=b):
                 if b == 0:
@@ -165,7 +167,7 @@
                 to_far[b].wait_recv()
                 relay[b].start()
 
-    for copy in (keep_p, keep_k, keep_v, keep_x):
+    for copy in (keep_p, keep_k, keep_v, keep_x, keep_next):
         copy.wait()
     for copy in (far_p, *to_far):
         copy.wait_send()
@@ -175,22 +177,23 @@
 
 def front(hidden, gain, rope, pos, w_key, w_value, w_query):
     rows, width = hidden.shape
-    half, kvw, qw = rows // 2, w_key.shape[1], w_query.shape[1]
+    half, part, kvw, qw = rows // 2, rows // 4, w_key.shape[1], w_query.shape[1]
     bf16 = jnp.bfloat16
     return pl.pallas_call(
         front_kernel,
         out_shape=(
-            jax.ShapeDtypeStruct((half, qw), bf16),
+            jax.ShapeDtypeStruct((part, qw), bf16),
             jax.ShapeDtypeStruct((rows, HEAD), jnp.float32),
             jax.ShapeDtypeStruct((rows, HEAD), jnp.float32),
             jax.ShapeDtypeStruct((rows, kvw), bf16),
+            jax.ShapeDtypeStruct((part, width), bf16),
             jax.ShapeDtypeStruct((half, width), bf16),
             jax.ShapeDtypeStruct((4, rows, kvw), bf16),
             jax.ShapeDtypeStruct((4, kvw, rows), bf16),
             jax.ShapeDtypeStruct((4, *pos.shape), jnp.int32),
         ),
         in_specs=[ANY, VMEM, VMEM, VMEM, ANY, ANY, ANY],
-        out_specs=(VMEM, VMEM, VMEM, VMEM, ANY, ANY, ANY, ANY),
+        out_specs=(VMEM, VMEM, VMEM, VMEM, ANY, ANY, ANY, ANY, ANY),
         scratch_shapes=[
             pltpu.VMEM((rows, width), bf16),
             pltpu.VMEM((rows, width), bf16),
@@ -199,7 +202,7 @@
             pltpu.VMEM((kvw, rows), bf16),
             pltpu.SemaphoreType.DMA((4,)),
             pltpu.SemaphoreType.DMA((SLOTS,)),
-            pltpu.SemaphoreType.DMA((4,)),
+            pltpu.SemaphoreType.DMA((5,)),
             pltpu.SemaphoreType.DMA((3 + 6 * kvw // STEP,)),
             pltpu.SemaphoreType.DMA((3 + 6 * kvw // STEP,)),
         ],
@@ -210,10 +213,10 @@
 
 def attn_kernel(lead, row_ref, q_ref, cos_ref, sin_ref, qpos_ref, kpos_ref, k_ref, vt_ref, token_ref, *rest):
     if lead:
-        w_ref, o_ref, part_ref, kp_s, q_s, s_s, m_s, l_s, acc_s, min_s, w_s, ctx_s, w_sem = rest
+        w_ref, o_ref, part_ref, kp_s, q_s, s_s, m_s, l_s, acc_s, w_s, ctx_s, w_sem = rest
         load = pltpu.make_async_copy(w_ref.at[:, 0:lead], w_s, w_sem)
     else:
-        o_ref, kp_s, q_s, s_s, m_s, l_s, acc_s, min_s = rest
+        o_ref, kp_s, q_s, s_s, m_s, l_s, acc_s = rest
     blocks, rows = k_ref.shape[0], k_ref.shape[1]
     groups, wide = acc_s.shape[0], acc_s.shape[2]
     pair = wide // Q_ROWS
@@ -227,9 +230,7 @@
         for b in range(blocks):
             for n in range(span):
                 kp_s[b, n * HEAD:(n + 1) * HEAD, :] = jnp.broadcast_to(kpos_ref[b * span + n:b * span + n + 1, :], (HEAD, HEAD)).T
-            min_s[b] = jnp.min(kpos_ref[b * span:(b + 1) * span, :])
-
-    min_s[blocks] = jnp.max(qpos)
+
     for g in range(groups * pair):
         x = q_ref[:, g * HEAD:(g + 1) * HEAD].astype(jnp.float32)
         q_s[g // pair, (g % pair) * Q_ROWS:(g % pair + 1) * Q_ROWS, :] = rotate(x, cos_ref[...], sin_ref[...])
@@ -237,30 +238,24 @@
     l_s[...] = jnp.zeros_like(l_s)
     acc_s[...] = jnp.zeros_like(acc_s)
 
-    @pl.loop(0, blocks)
-    def _(b):
-        @pl.when(min_s[b] <= min_s[blocks])
-        def _():
-            k = k_ref[b]
-            allowed = jnp.concatenate([kp_s[b] <= qpos] * pair, axis=1)
-            for g in range(groups):
-                s = lax.dot_general(k, q_s[g], (((1,), (1,)), ((), ())), preferred_element_type=jnp.float32)
-                s = jnp.where(allowed, s, NEG_BIG)
-                s_s[b, g] = s
-                m_s[g] = jnp.maximum(m_s[g], jnp.max(s.reshape(rows // 8, 8, wide), axis=0))
+    for b in range(blocks):
+        k = k_ref[b]
+        allowed = jnp.concatenate([kp_s[b] <= qpos] * pair, axis=1)
+        for g in range(groups):
+            s = lax.dot_general(k, q_s[g], (((1,), (1,)), ((), ())), preferred_element_type=jnp.float32)
+            s = jnp.where(allowed, s, NEG_BIG)
+            s_s[b, g] = s
+            m_s[g] = jnp.maximum(m_s[g], jnp.max(s.reshape(rows // 8, 8, wide), axis=0))
 
     for g in range(groups):
         m_s[g] = jnp.broadcast_to(jnp.max(m_s[g], axis=0, keepdims=True), (8, wide)) * EXP_SCALE
 
-    @pl.loop(0, blocks)
-    def _(b):
-        @pl.when(min_s[b] <= min_s[blocks])
-        def _():
-            vt = vt_ref[b]
-            for g in range(groups):
-                p = jnp.exp2(s_s[b, g].reshape(rows // 8, 8, wide) * EXP_SCALE - m_s[g][None])
-                l_s[g] += jnp.sum(p, axis=0)
-                acc_s[g] += dot(vt, p.reshape(rows, wide).astype(jnp.bfloat16))
+    for b in range(blocks):
+        vt = vt_ref[b]
+        for g in range(groups):
+            p = jnp.exp2(s_s[b, g].reshape(rows // 8, 8, wide) * EXP_SCALE - m_s[g][None])
+            l_s[g] += jnp.sum(p, axis=0)
+            acc_s[g] += dot(vt, p.reshape(rows, wide).astype(jnp.bfloat16))
 
     for g in range(groups * pair):
         cols = slice((g % pair) * Q_ROWS, (g % pair + 1) * Q_ROWS)
@@ -277,34 +272,32 @@
             part_ref[...] = dot(ctx, w_s[...])
 
 
-def attention(q, r, count, cos, sin, pos, k_all, vt_all, kpos, block, token, w_out=None, lead=0):
+def attention(q, cos, sin, pos, k_all, vt_all, kpos, block, token, w_out=None, lead=0):
     blocks, brows, kvw = k_all.shape
-    width = q.shape[1]
-    rows = count * Q_ROWS
-    per = q.shape[0] // Q_ROWS
+    rows, width = q.shape
     kv = kvw // HEAD
     g = width // kvw
     wide = PAIR * Q_ROWS
-    table = pl.BlockSpec((Q_ROWS, HEAD), lambda n, s: (s[0] * per + r + lax.div(n, kv), 0))
-    unit = lambda first: pl.BlockSpec((Q_ROWS, g * HEAD), lambda n, s: (first + lax.div(n, kv), lax.rem(n, kv)))
+    table = pl.BlockSpec((Q_ROWS, HEAD), lambda n, s: (s[0] + lax.div(n, kv), 0))
+    unit = pl.BlockSpec((Q_ROWS, g * HEAD), lambda n, s: (lax.div(n, kv), lax.rem(n, kv)))
     return pl.pallas_call(
         functools.partial(attn_kernel, lead),
         out_shape=(jax.ShapeDtypeStruct((rows, width), jnp.bfloat16), *([jax.ShapeDtypeStruct((rows, lead), jnp.float32)] if lead else [])),
         grid_spec=pltpu.PrefetchScalarGridSpec(
             num_scalar_prefetch=1,
-            grid=(count * kv,),
+            grid=(rows // Q_ROWS * kv,),
             in_specs=[
-                unit(r),
+                unit,
                 table,
                 table,
-                pl.BlockSpec((None, 1, HEAD), lambda n, s: (s[0] * per + r + lax.div(n, kv), 0, 0)),
+                pl.BlockSpec((None, 1, HEAD), lambda n, s: (s[0] + lax.div(n, kv), 0, 0)),
                 pl.BlockSpec(kpos.shape, lambda n, s: (0, 0)),
                 pl.BlockSpec((blocks, brows, HEAD), lambda n, s: (0, 0, lax.rem(n, kv))),
                 pl.BlockSpec((blocks, HEAD, brows), lambda n, s: (0, lax.rem(n, kv), 0)),
                 ANY,
                 *([ANY] if lead else []),
             ],
-            out_specs=(unit(0), *([pl.BlockSpec((rows, lead), lambda n, s: (0, 0))] if lead else [])),
+            out_specs=(unit, *([pl.BlockSpec((rows, lead), lambda n, s: (0, 0))] if lead else [])),
             scratch_shapes=[
                 pltpu.VMEM((blocks, brows, HEAD), jnp.int32),
                 pltpu.VMEM((g // PAIR, wide, HEAD), jnp.bfloat16),
@@ -312,7 +305,6 @@
                 pltpu.VMEM((g // PAIR, 8, wide), jnp.float32),
                 pltpu.VMEM((g // PAIR, 8, wide), jnp.float32),
                 pltpu.VMEM((g // PAIR, HEAD, wide), jnp.float32),
-                pltpu.SMEM((blocks + 1,), jnp.int32),
                 *([pltpu.VMEM((width, lead), jnp.bfloat16), pltpu.VMEM((kv, Q_ROWS, g * HEAD), jnp.bfloat16), pltpu.SemaphoreType.DMA] if lead else []),
             ],
         ),
@@ -427,24 +419,25 @@
 
     def local_block(hidden, tok_pos, norm_gain, w_query, w_key, w_value, w_out):
         rows, _ = hidden.shape
-        half = rows // 2
         kv = w_key.shape[1] // HEAD
         t = lax.axis_index("tp").astype(jnp.int32)
         own, send = t[None], 1 - t[None]
         pos = tok_pos.reshape(-1, HEAD)
-        q, cos, sin, v, own_x, k_all, vt_all, p_all = front(hidden, norm_gain[None, :], rope_rows(), pos, w_key, w_value, w_query)
+        q, cos, sin, v, next_x, own_x, k_all, vt_all, p_all = front(hidden, norm_gain[None, :], rope_rows(), pos, w_key, w_value, w_query)
         kpos = p_all.reshape(-1, HEAD)
         chunks = [(a, b - a) for a, b in zip(CUTS, CUTS[1:])]
         token = q
         parts = []
-        for r in range(half // Q_ROWS):
-            (ctx, token), part = then_send(attention, q, r, 1, cos, sin, pos, k_all, vt_all, kpos, send, token, w_out, CUTS[1])
+        for r in range(2):
+            if r > 0:
+                token = q = project_q(next_x, w_query, token)
+            (ctx, token), part = then_send(attention, q, cos, sin, pos, k_all, vt_all, kpos, 2 * send + r, token, w_out, CUTS[1])
             parts.append([part])
             for start, cols in chunks[1:]:
                 token, part = then_send(project_out, ctx, w_out, start, cols, token)
                 parts[r].append(part)
         q = project_q(own_x, w_query, token)
-        ctx = attention(q, 0, half // Q_ROWS, cos, sin, pos, k_all, vt_all, kpos, own, q)[0]
+        ctx = attention(q, cos, sin, pos, k_all, vt_all, kpos, 2 * own, q)[0]
         out = None
         others = []
         for c, (start, cols) in enumerate(chunks):

time: 366 us -> 396 us (1.082)
  the two profiles are of different devices: /device:TPU:2 before, /device:TPU:0 now
where the time goes in v1:
time: 396 us; the launch traced here: 395 us
  Pallas kernels  269 us (68%)
  waiting for transfers between devices  105 us (27%)
  starting transfers between devices  13.6 us (3%)
  local copies, waits for them, and re-layouts  6.24 us (2%)
    ppermute x15, waiting for transfers between devices, then_send(): return (got, lax.ppermute(out, 'tp', swap_tp))  105 us
    pallas_call x8, Pallas kernels, project_out(): pl.pallas_call(part_kernel, out_shape=jax.ShapeDtypeStruct((rows, cols),...  62.6 us
    pallas_call x3, Pallas kernels, attention(): pl.pallas_call(functools.partial(attn_kernel, lead), out_shape=(jax.Shape...  62.1 us
    pallas_call x2, Pallas kernels, project_q(): pl.pallas_call(q_kernel, out_shape=jax.ShapeDtypeStruct((rows, width), jn...  51.8 us
    pallas_call x5, Pallas kernels, finish(): pl.pallas_call(final_kernel, out_shape=(jax.ShapeDtypeStruct((rows, cols)...  46.8 us
    pallas_call x1, Pallas kernels, front(): pl.pallas_call(front_kernel, out_shape=(jax.ShapeDtypeStruct((part, qw),...  39.3 us
    ppermute x15, starting transfers between devices, then_send(): return (got, lax.ppermute(out, 'tp', swap_tp))  13.6 us
  transfers between devices with their start and end apart: 15, of which 4 were waited for; matrix products, arithmetic and copies ran while one was open for 1% of the time, Pallas kernels for 50%

profile of v1, /device:TPU:0, one launch (start us, length us, event | category | flops | bytes accessed | tf_op | source)
XLA Modules:
  0.0 395.3 jit_solution(5071820431764072668)
XLA Ops:
  0.7 0.6 pad_maximum_fusion.rope_ref
  1.2 39.3 %shard_map.94 = (bf16[128,4096]{1,0:T(8,128)(2,1)}, f32[512,128]{1,0:T(8,128)}, f32[512,128]{1,0:T(8,128)}, bf16[512,512]{1,0:T(8,128)(2,1)}, bf16[128,8192]{1,0...) custom-call(bf16[512,8192]{1,0:T(8,128)(2,1)} %hid_ref.11, ...), custom_call_target="tpu_custom_call" | custom-call | flops 25769803776 | bytes 92274688 | tf_op jit(solution)/shard_map/pallas_call | solution.py:182
  40.6 16.9 %shard_map.95 = (bf16[128,4096]{1,0:T(8,128)(2,1)}, f32[128,1024]{1,0:T(8,128)}) custom-call(s32[1]{0:T(128)S(6)} %mul.23.row_ref, bf16[128,4096]{1,0:T(8,128)(2,1)} %get-tuple-element.28.q_ref.token_ref, f32[512,128]{1,0:T(8,128)} %get-tuple-element.29.cos_ref, f32[512,128]{1,0:T(8,128)} %get-tuple-element.30.sin_ref, s32[4,1,128]{2,1,0:T(1,128)} %bitcast.9, ...), custom_call_target="tpu_custom_call" | custom-call | flops 4294967296 | bytes 2097152 | tf_op jit(solution)/shard_map/pallas_call | solution.py:283
  57.5 1.5 collective-permute-start.8
  59.0 8.5 %shard_map.96.token_ref = f32[128,2048]{1,0:T(8,128)} custom-call(bf16[128,4096]{1,0:T(8,128)(2,1)} %get-tuple-element.34.x_ref, bf16[4096,8192]{1,0:T(8,128)(2,1)} %w_ref.29, f32[128,1024]{1,0:T(8,128)} %get-tuple-element.35.token_ref), custom_call_target="tpu_custom_call" | custom-call | flops 2147483648 | bytes 17825792 | tf_op jit(solution)/shard_map/pallas_call | solution.py:338
  67.5 0.5 collective-permute-start.6
  68.0 8.5 %shard_map.97.token_ref = f32[128,2048]{1,0:T(8,128)} custom-call(bf16[128,4096]{1,0:T(8,128)(2,1)} %get-tuple-element.34.x_ref, bf16[4096,8192]{1,0:T(8,128)(2,1)} %w_ref.29, f32[128,2048]{1,0:T(8,128)} %shard_map.96.token_ref), custom_call_target="tpu_custom_call" | custom-call | flops 2147483648 | bytes 17825792 | tf_op jit(solution)/shard_map/pallas_call | solution.py:338
  76.6 1.5 collective-permute-start.4
  78.1 10.3 %shard_map.98.token_ref = f32[128,2560]{1,0:T(8,128)} custom-call(bf16[128,4096]{1,0:T(8,128)(2,1)} %get-tuple-element.34.x_ref, bf16[4096,8192]{1,0:T(8,128)(2,1)} %w_ref.29, f32[128,2048]{1,0:T(8,128)} %shard_map.97.token_ref), custom_call_target="tpu_custom_call" | custom-call | flops 2684354560 | bytes 22020096 | tf_op jit(solution)/shard_map/pallas_call | solution.py:338
  88.4 3.9 shard_map.99.token_ref
  92.3 23.4 %shard_map.100.q_ref.token_ref = bf16[128,4096]{1,0:T(8,128)(2,1)} custom-call(bf16[128,8192]{1,0:T(8,128)(2,1)} %get-tuple-element.27.x_ref, bf16[8192,4096]{1,0:T(8,128)(2,1)} %w_ref.24, f32[128,512]{1,0:T(8,128)} %shard_map.99.token_ref), custom_call_target="tpu_custom_call" | custom-call | flops 8589934592 | bytes 69206016 | tf_op jit(solution)/shard_map/pallas_call | solution.py:322
  115.8 16.9 %shard_map.101 = (bf16[128,4096]{1,0:T(8,128)(2,1)}, f32[128,1024]{1,0:T(8,128)}) custom-call(s32[1]{0:T(128)S(6)} %add.17.row_ref, bf16[128,4096]{1,0:T(8,128)(2,1)} %shard_map.100.q_ref.token_ref, f32[512,128]{1,0:T(8,128)} %get-tuple-element.29.cos_ref, f32[512,128]{1,0:T(8,128)} %get-tuple-element.30.sin_ref, s32[4,1,128]{2,1,0:T(1,128)} %bitcast.10, ...), custom_call_target="tpu_custom_call" | custom-call | flops 4294967296 | bytes 2097152 | tf_op jit(solution)/shard_map/pallas_call | solution.py:283
  132.7 0.5 collective-permute-start.9
  133.2 8.5 %shard_map.102.token_ref = f32[128,2048]{1,0:T(8,128)} custom-call(bf16[128,4096]{1,0:T(8,128)(2,1)} %get-tuple-element.36.x_ref, bf16[4096,8192]{1,0:T(8,128)(2,1)} %w_ref.29, f32[128,1024]{1,0:T(8,128)} %get-tuple-element.37.token_ref), custom_call_target="tpu_custom_call" | custom-call | flops 2147483648 | bytes 17825792 | tf_op jit(solution)/shard_map/pallas_call | solution.py:338
  141.7 1.5 collective-permute-start.7
  143.2 8.5 %shard_map.103.token_ref = f32[128,2048]{1,0:T(8,128)} custom-call(bf16[128,4096]{1,0:T(8,128)(2,1)} %get-tuple-element.36.x_ref, bf16[4096,8192]{1,0:T(8,128)(2,1)} %w_ref.29, f32[128,2048]{1,0:T(8,128)} %shard_map.102.token_ref), custom_call_target="tpu_custom_call" | custom-call | flops 2147483648 | bytes 17825792 | tf_op jit(solution)/shard_map/pallas_call | solution.py:338
  151.7 10.3 %shard_map.104.token_ref = f32[128,2560]{1,0:T(8,128)} custom-call(bf16[128,4096]{1,0:T(8,128)(2,1)} %get-tuple-element.36.x_ref, bf16[4096,8192]{1,0:T(8,128)(2,1)} %w_ref.29, f32[128,2048]{1,0:T(8,128)} %shard_map.103.token_ref), custom_call_target="tpu_custom_call" | custom-call | flops 2684354560 | bytes 22020096 | tf_op jit(solution)/shard_map/pallas_call | solution.py:338
  162.1 4.0 %shard_map.105.token_ref = f32[128,512]{1,0:T(8,128)} custom-call(bf16[128,4096]{1,0:T(8,128)(2,1)} %get-tuple-element.36.x_ref, bf16[4096,8192]{1,0:T(8,128)(2,1)} %w_ref.29, f32[128,2560]{1,0:T(8,128)} %shard_map.104.token_ref), custom_call_target="tpu_custom_call" | custom-call | flops 536870912 | bytes 5242880 | tf_op jit(solution)/shard_map/pallas_call | solution.py:338
  166.0 28.4 %shard_map.106.q_ref.token_ref = bf16[256,4096]{1,0:T(8,128)(2,1)} custom-call(bf16[256,8192]{1,0:T(8,128)(2,1)} %get-tuple-element.26.x_ref, bf16[8192,4096]{1,0:T(8,128)(2,1)} %w_ref.24, f32[128,512]{1,0:T(8,128)} %shard_map.105.token_ref), custom_call_target="tpu_custom_call" | custom-call | flops 17179869184 | bytes 71303168 | tf_op jit(solution)/shard_map/pallas_call | solution.py:322
  194.4 0.5 collective-permute-start.5
  194.9 1.5 collective-permute-start.3
  196.5 0.5 collective-permute-start.2
  197.0 28.3 %shard_map.107.x_ref = bf16[256,4096]{1,0:T(8,128)(2,1)} custom-call(s32[1]{0:T(128)S(6)} %mul.20.row_ref, bf16[256,4096]{1,0:T(8,128)(2,1)} %shard_map.106.q_ref.token_ref, f32[512,128]{1,0:T(8,128)} %get-tuple-element.29.cos_ref, f32[512,128]{1,0:T(8,128)} %get-tuple-element.30.sin_ref, s32[4,1,128]{2,1,0:T(1,128)} %bitcast.11, s32[16,128]{1,0:T(8,128)} %bitcast.7, ...), custom_call_target="tpu_custom_call" | custom-call | flops 8589934592 | bytes 4194304 | tf_op jit(solution)/shard_map/pallas_call | solution.py:283
  225.3 6.6 %shard_map.108 = (bf16[256,1024]{1,0:T(8,128)(2,1)}, bf16[512,8192]{1,0:T(8,128)(2,1)}) custom-call(s32[1]{0:T(128)} %bitcast.row_ref, bf16[256,4096]{1,0:T(8,128)(2,1)} %shard_map.107.x_ref, bf16[4096,8192]{1,0:T(8,128)(2,1)} %w_ref.29, bf16[512,8192]{1,0:T(8,128)(2,1)} %hid_ref.11, f32[128,1024]{1,0:T(8,128)} %collective-permute-done.8.pa_ref, ...), custom_call_target="tpu_custom_call" | custom-call | flops 2147483648 | bytes 10485760 | tf_op jit(solution)/shard_map/pallas_call | solution.py:364
  231.9 11.0 %shard_map.109 = (bf16[256,2048]{1,0:T(8,128)(2,1)}, bf16[512,8192]{1,0:T(8,128)(2,1)}) custom-call(s32[1]{0:T(128)} %bitcast.row_ref, bf16[256,4096]{1,0:T(8,128)(2,1)} %shard_map.107.x_ref, bf16[4096,8192]{1,0:T(8,128)(2,1)} %w_ref.29, bf16[512,8192]{1,0:T(8,128)(2,1)} %hid_ref.11, ...), custom_call_target="tpu_custom_call", output_to_operand_aliasing={{1}: (6, {})} | custom-call | flops 4294967296 | bytes 18874368 | tf_op jit(solution)/shard_map/pallas_call | solution.py:364
  242.9 11.0 %shard_map.110 = (bf16[256,2048]{1,0:T(8,128)(2,1)}, bf16[512,8192]{1,0:T(8,128)(2,1)}) custom-call(s32[1]{0:T(128)} %bitcast.row_ref, bf16[256,4096]{1,0:T(8,128)(2,1)} %shard_map.107.x_ref, bf16[4096,8192]{1,0:T(8,128)(2,1)} %w_ref.29, bf16[512,8192]{1,0:T(8,128)(2,1)} %hid_ref.11, ...), custom_call_target="tpu_custom_call", output_to_operand_aliasing={{1}: (6, {})} | custom-call | flops 4294967296 | bytes 18874368 | tf_op jit(solution)/shard_map/pallas_call | solution.py:364
  253.8 21.1 %collective-permute-done.2.pa_ref = f32[128,2560]{1,0:T(8,128)} collective-permute-done((f32[128,2560]{1,0:T(8,128)S(1)}, f32[128,2560]{1,0:T(8,128)}, u32[]{:S(2)}, u32[]{:S(2)}) %collective-permute-start.2) | collective-permute-done | bytes 1310752 | tf_op jit(solution)/shard_map/ppermute | solution.py:418
  275.0 13.2 %shard_map.111 = (bf16[256,2560]{1,0:T(8,128)(2,1)}, bf16[512,8192]{1,0:T(8,128)(2,1)}) custom-call(s32[1]{0:T(128)} %bitcast.row_ref, bf16[256,4096]{1,0:T(8,128)(2,1)} %shard_map.107.x_ref, bf16[4096,8192]{1,0:T(8,128)(2,1)} %w_ref.29, bf16[512,8192]{1,0:T(8,128)(2,1)} %hid_ref.11, ...), custom_call_target="tpu_custom_call", output_to_operand_aliasing={{1}: (6, {})} | custom-call | flops 5368709120 | bytes 23068672 | tf_op jit(solution)/shard_map/pallas_call | solution.py:364
  288.2 0.5 collective-permute-start.14
  288.7 1.6 collective-permute-start.13
  290.2 0.5 collective-permute-start.12
  290.7 1.6 collective-permute-start
  292.3 0.5 collective-permute-start.1
  292.7 77.9 %collective-permute-done.pa_ref = f32[128,512]{1,0:T(8,128)S(1)} collective-permute-done((f32[128,512]{1,0:T(8,128)S(1)}, f32[128,512]{1,0:T(8,128)S(1)}, u32[]{:S(2)}, u32[]{:S(2)}) %collective-permute-start) | collective-permute-done | bytes 262176 | tf_op jit(solution)/shard_map/ppermute | solution.py:418
  370.6 0.5 collective-permute-start.11
  371.1 5.1 %collective-permute-done.1.pb_ref = f32[128,512]{1,0:T(8,128)S(1)} collective-permute-done((f32[128,512]{1,0:T(8,128)S(1)}, f32[128,512]{1,0:T(8,128)S(1)}, u32[]{:S(2)}, u32[]{:S(2)}) %collective-permute-start.1) | collective-permute-done | bytes 262176 | tf_op jit(solution)/shard_map/ppermute | solution.py:418
  376.3 0.7 copy-done.9
  377.0 5.0 %shard_map.112 = (bf16[256,512]{1,0:T(8,128)(2,1)}, bf16[512,8192]{1,0:T(8,128)(2,1)}) custom-call(s32[1]{0:T(128)} %bitcast.row_ref, bf16[256,4096]{1,0:T(8,128)(2,1)} %shard_map.107.x_ref, bf16[4096,8192]{1,0:T(8,128)(2,1)} %w_ref.29, bf16[512,8192]{1,0:T(8,128)(2,1)} %hid_ref.11, f32[128,512]{1,0:T(8,128)} %copy-done.8, ...), custom_call_target="tpu_custom_call", output_to_operand_aliasing={{1}: (6, {})} | custom-call | flops 1073741824 | bytes 6291456 | tf_op jit(solution)/shard_map/pallas_call | solution.py:364
  382.0 0.5 collective-permute-start.10
  382.4 1.1 slice.3
  383.5 2.0 reshape.64
  385.5 0.9 reshape_squeeze.3
  386.4 1.1 collective-permute-done.11.refs_0_
  387.5 0.8 copy-done.7
  388.3 0.3 copy-done.5
  388.6 0.4 copy-done.2
  389.1 4.5 %shard_map.113.refs_1_ = bf16[512,8192]{1,0:T(8,128)(2,1)} custom-call(s32[1]{0:T(128)S(6)} %sub.3.row_ref, bf16[256,1024]{1,0:T(8,128)(2,1)} %copy-done.7, bf16[256,2048]{1,0:T(8,128)(2,1)} %collective-permute-done.12.refs_1_, bf16[256,2048]{1,0:T(8,128)(2,1)} %copy-done.5, bf16[256,2560]{1,0:T(8,128)(2,1)} %copy-done.2, ...), custom_call_target="tpu_custom_call", output_to_operand_aliasing={{}: (5, {})} | custom-call | bytes 7864320 | tf_op jit(solution)/shard_map/pallas_call | solution.py:398
  393.6 1.7 shard_map.114
  (28 shorter events, 0.1 us)
Async XLA Ops:
  57.5 136.9 %collective-permute-start.8 = (f32[128,1024]{1,0:T(8,128)}, f32[128,1024]{1,0:T(8,128)}, u32[]{:S(2)}, u32[]{:S(2)}) collective-permute-start(f32[128,1024]{1,0:T(8,128)} %get-tuple-element.35.token_ref), channel_id=1, source_target_pairs={{0,4},{4,0},{1,5},{5,1},{2,6},{6,2},{3,7},{7,3}} | collective-permute-start | bytes 1572872 | tf_op jit(solution)/shard_map/ppermute | solution.py:418
  67.5 128.9 %collective-permute-start.6 = (f32[128,2048]{1,0:T(8,128)}, f32[128,2048]{1,0:T(8,128)}, u32[]{:S(2)}, u32[]{:S(2)}) collective-permute-start(f32[128,2048]{1,0:T(8,128)} %shard_map.96.token_ref), channel_id=1, source_target_pairs={{0,4},{4,0},{1,5},{5,1},{2,6},{6,2},{3,7},{7,3}} | collective-permute-start | bytes 3145736 | tf_op jit(solution)/shard_map/ppermute | solution.py:418
  76.6 166.3 %collective-permute-start.4 = (f32[128,2048]{1,0:T(8,128)}, f32[128,2048]{1,0:T(8,128)}, u32[]{:S(2)}, u32[]{:S(2)}) collective-permute-start(f32[128,2048]{1,0:T(8,128)} %shard_map.97.token_ref), channel_id=1, source_target_pairs={{0,4},{4,0},{1,5},{5,1},{2,6},{6,2},{3,7},{7,3}} | collective-permute-start | bytes 3145736 | tf_op jit(solution)/shard_map/ppermute | solution.py:418
  132.7 62.2 %collective-permute-start.9 = (f32[128,1024]{1,0:T(8,128)}, f32[128,1024]{1,0:T(8,128)S(1)}, u32[]{:S(2)}, u32[]{:S(2)}) collective-permute-start(f32[128,1024]{1,0:T(8,128)} %get-tuple-element.37.token_ref), channel_id=1, source_target_pairs={{0,4},{4,0},{1,5},{5,1},{2,6},{6,2},{3,7},{7,3}} | collective-permute-start | bytes 1572872 | tf_op jit(solution)/shard_map/ppermute | solution.py:418
  141.7 90.1 %collective-permute-start.7 = (f32[128,2048]{1,0:T(8,128)}, f32[128,2048]{1,0:T(8,128)}, u32[]{:S(2)}, u32[]{:S(2)}) collective-permute-start(f32[128,2048]{1,0:T(8,128)} %shard_map.102.token_ref), channel_id=1, source_target_pairs={{0,4},{4,0},{1,5},{5,1},{2,6},{6,2},{3,7},{7,3}} | collective-permute-start | bytes 3145736 | tf_op jit(solution)/shard_map/ppermute | solution.py:418
  166.0 28.9 %copy-start.1 = (f32[128,2560]{1,0:T(8,128)S(1)}, f32[128,2560]{1,0:T(8,128)}, u32[]{:S(2)}) copy-start(f32[128,2560]{1,0:T(8,128)} %shard_map.104.token_ref) | copy-start | bytes 3932164
  166.0 30.4 %copy-start = (f32[128,2560]{1,0:T(8,128)S(1)}, f32[128,2560]{1,0:T(8,128)}, u32[]{:S(2)}) copy-start(f32[128,2560]{1,0:T(8,128)} %shard_map.98.token_ref) | copy-start | bytes 3932164
  194.4 48.5 %collective-permute-start.5 = (f32[128,2048]{1,0:T(8,128)}, f32[128,2048]{1,0:T(8,128)}, u32[]{:S(2)}, u32[]{:S(2)}) collective-permute-start(f32[128,2048]{1,0:T(8,128)} %shard_map.103.token_ref), channel_id=1, source_target_pairs={{0,4},{4,0},{1,5},{5,1},{2,6},{6,2},{3,7},{7,3}} | collective-permute-start | bytes 3145736 | tf_op jit(solution)/shard_map/ppermute | solution.py:418
  194.9 30.4 %copy-start.6 = (f32[128,1024]{1,0:T(8,128)}, f32[128,1024]{1,0:T(8,128)S(1)}, u32[]{:S(2)}) copy-start(f32[128,1024]{1,0:T(8,128)S(1)} %collective-permute-done.9.pb_ref) | copy-start | bytes 1572868
  194.9 58.9 %collective-permute-start.3 = (f32[128,2560]{1,0:T(8,128)S(1)}, f32[128,2560]{1,0:T(8,128)}, u32[]{:S(2)}, u32[]{:S(2)}) collective-permute-start(f32[128,2560]{1,0:T(8,128)S(1)} %copy-done.1), channel_id=1, source_target_pairs={{0,4},{4,0},{1,5},{5,1},{2,6},{6,2},{3,7},{7,3}} | collective-permute-start | bytes 3932168 | tf_op jit(solution)/shard_map/ppermute | solution.py:418
  196.5 78.5 %collective-permute-start.2 = (f32[128,2560]{1,0:T(8,128)S(1)}, f32[128,2560]{1,0:T(8,128)}, u32[]{:S(2)}, u32[]{:S(2)}) collective-permute-start(f32[128,2560]{1,0:T(8,128)S(1)} %copy-done), channel_id=1, source_target_pairs={{0,4},{4,0},{1,5},{5,1},{2,6},{6,2},{3,7},{7,3}} | collective-permute-start | bytes 3932168 | tf_op jit(solution)/shard_map/ppermute | solution.py:418
  275.0 15.8 %copy-start.3 = (f32[128,512]{1,0:T(8,128)S(1)}, f32[128,512]{1,0:T(8,128)}, u32[]{:S(2)}) copy-start(f32[128,512]{1,0:T(8,128)} %shard_map.99.token_ref) | copy-start | bytes 786436
  275.0 17.3 %copy-start.4 = (f32[128,512]{1,0:T(8,128)S(1)}, f32[128,512]{1,0:T(8,128)}, u32[]{:S(2)}) copy-start(f32[128,512]{1,0:T(8,128)} %shard_map.105.token_ref) | copy-start | bytes 786436
  288.2 99.3 %collective-permute-start.14 = (bf16[256,2560]{1,0:T(8,128)(2,1)}, bf16[256,2560]{1,0:T(8,128)(2,1)S(1)}, u32[]{:S(2)}, u32[]{:S(2)}) collective-permute-start(bf16[256,2560]{1,0:T(8,128)(2,1)} %get-tuple-element.46), channel_id=1, source_target_pairs={{0,4},{4,0},{1,5},{5,1},{2,6},{6,2},{3,7},{7,3}} | collective-permute-start | bytes 3932168 | tf_op jit(solution)/shard_map/ppermute | solution.py:418
  288.7 98.8 %collective-permute-start.13 = (bf16[256,2048]{1,0:T(8,128)(2,1)}, bf16[256,2048]{1,0:T(8,128)(2,1)S(1)}, u32[]{:S(2)}, u32[]{:S(2)}) collective-permute-start(bf16[256,2048]{1,0:T(8,128)(2,1)} %get-tuple-element.45), channel_id=1, source_target_pairs={{0,4},{4,0},{1,5},{5,1},{2,6},{6,2},{3,7},{7,3}} | collective-permute-start | bytes 3145736 | tf_op jit(solution)/shard_map/ppermute | solution.py:418
  290.2 97.2 %collective-permute-start.12 = (bf16[256,2048]{1,0:T(8,128)(2,1)}, bf16[256,2048]{1,0:T(8,128)(2,1)}, u32[]{:S(2)}, u32[]{:S(2)}) collective-permute-start(bf16[256,2048]{1,0:T(8,128)(2,1)} %get-tuple-element.44), channel_id=1, source_target_pairs={{0,4},{4,0},{1,5},{5,1},{2,6},{6,2},{3,7},{7,3}} | collective-permute-start | bytes 3145736 | tf_op jit(solution)/shard_map/ppermute | solution.py:418
  290.7 79.9 %collective-permute-start = (f32[128,512]{1,0:T(8,128)S(1)}, f32[128,512]{1,0:T(8,128)S(1)}, u32[]{:S(2)}, u32[]{:S(2)}) collective-permute-start(f32[128,512]{1,0:T(8,128)S(1)} %copy-done.3), channel_id=1, source_target_pairs={{0,4},{4,0},{1,5},{5,1},{2,6},{6,2},{3,7},{7,3}} | collective-permute-start | bytes 786440 | tf_op jit(solution)/shard_map/ppermute | solution.py:418
  292.3 84.0 %collective-permute-start.1 = (f32[128,512]{1,0:T(8,128)S(1)}, f32[128,512]{1,0:T(8,128)S(1)}, u32[]{:S(2)}, u32[]{:S(2)}) collective-permute-start(f32[128,512]{1,0:T(8,128)S(1)} %copy-done.4), channel_id=1, source_target_pairs={{0,4},{4,0},{1,5},{5,1},{2,6},{6,2},{3,7},{7,3}} | collective-permute-start | bytes 786440 | tf_op jit(solution)/shard_map/ppermute | solution.py:418
  370.6 5.6 %copy-start.8 = (f32[128,512]{1,0:T(8,128)}, f32[128,512]{1,0:T(8,128)S(1)}, u32[]{:S(2)}) copy-start(f32[128,512]{1,0:T(8,128)S(1)} %collective-permute-done.pa_ref) | copy-start | bytes 786436
  370.6 16.8 %collective-permute-start.11 = (bf16[256,1024]{1,0:T(8,128)(2,1)}, bf16[256,1024]{1,0:T(8,128)(2,1)S(1)}, u32[]{:S(2)}, u32[]{:S(2)}) collective-permute-start(bf16[256,1024]{1,0:T(8,128)(2,1)} %get-tuple-element.43), channel_id=1, source_target_pairs={{0,4},{4,0},{1,5},{5,1},{2,6},{6,2},{3,7},{7,3}} | collective-permute-start | bytes 1572872 | tf_op jit(solution)/shard_map/ppermute | solution.py:418
  376.2 0.7 copy-start.9
  382.0 11.6 %collective-permute-start.10 = (bf16[256,512]{1,0:T(8,128)(2,1)}, bf16[256,512]{1,0:T(8,128)(2,1)}, u32[]{:S(2)}, u32[]{:S(2)}) collective-permute-start(bf16[256,512]{1,0:T(8,128)(2,1)} %get-tuple-element.42), channel_id=1, source_target_pairs={{0,4},{4,0},{1,5},{5,1},{2,6},{6,2},{3,7},{7,3}} | collective-permute-start | bytes 786440 | tf_op jit(solution)/shard_map/ppermute | solution.py:418
  387.5 0.8 copy-start.7
  387.5 1.2 copy-start.5
  387.5 1.6 copy-start.2

commit v2 on v1

--- a/solution.py
+++ b/solution.py
@@ -1,4 +1,5 @@
 import functools
+import math
 
 import jax
 import jax.numpy as jnp
@@ -76,13 +77,31 @@
     far_p, core_p = send(0, pos_ref, pall_ref.at[2], far), send(1, pos_ref, pall_ref.at[1], core)
     relay_p = send(2, pall_ref.at[2], pall_ref.at[3], core)
     to_far, to_core, relay = [], [], []
-    for b in range(first_q):
+    pieces = [(0, pl.ds(0, half)), (0, pl.ds(half, half)), *((b, pl.ds(0, rows)) for b in range(1, first_q))]
+    for n, (b, r) in enumerate(pieces):
         cut = pl.ds((b % nk) * STEP, STEP)
-        at = (slice(None), cut) if b < nk else (cut, slice(None))
+        at = (r, cut) if b < nk else (cut, r)
         src, dst = (k_s, kall_ref) if b < nk else (vt_s, vall_ref)
-        to_far.append(send(3 + 3 * b, src.at[at], dst.at[(2, *at)], far))
-        to_core.append(send(4 + 3 * b, src.at[at], dst.at[(1, *at)], core))
-        relay.append(send(5 + 3 * b, dst.at[(2, *at)], dst.at[(3, *at)], core))
+        to_far.append(send(3 + 3 * n, src.at[at], dst.at[(2, *at)], far))
+        to_core.append(send(4 + 3 * n, src.at[at], dst.at[(1, *at)], core))
+        relay.append(send(5 + 3 * n, dst.at[(2, *at)], dst.at[(3, *at)], core))
+
+    def pass_on(n):
+        to_far[n].start()
+        to_core[n].start()
+
+    def project(b, j):
+        r = pl.ds(pl.multiple_of(j * half, half), half)
+        out = dot(x_s[r, :], w_s[b % SLOTS]).astype(jnp.bfloat16)
+        for h in range(STEP // HEAD):
+            piece = out[:, h * HEAD:(h + 1) * HEAD]
+            cols = pl.ds((b % nk) * STEP + h * HEAD, HEAD)
+            if b < nk:
+                k_s[r, cols] = rotate(piece.astype(jnp.float32), cos_ref[r, :], sin_ref[r, :])
+            else:
+                v_ref[r, cols] = piece
+                vt_s[cols, r] = piece.T
+
     keep_p = pltpu.make_async_copy(pos_ref, pall_ref.at[0], out_sem.at[0])
     keep_k = pltpu.make_async_copy(k_s, kall_ref.at[0], out_sem.at[1])
     keep_v = pltpu.make_async_copy(vt_s, vall_ref.at[0], out_sem.at[2])
@@ -99,10 +118,11 @@
     group = 64
     for c in range(4):
         loads[c].wait()
-        if c < 2:
-            loads[c + 2].start()
-        for b in ((), (), (0, 1), (2,))[c]:
-            weight(b).start()
+        (loads[2] if c == 1 else weight((0, 0, 1, 3)[c])).start()
+        if c == 2:
+            weight(2).start()
+        if c == 3:
+            weight(4).start()
 
         @pl.loop(0, part // group)
         def _(g, c=c):
@@ -117,26 +137,26 @@
                 cols = slice(j * HEAD, (j + 1) * HEAD)
                 x_s[r, cols] = (hid_s[r, cols].astype(jnp.float32) * inv * gain_ref[:, cols]).astype(jnp.bfloat16)
 
-    for b in range(first_q):
+        if c == 1:
+            weight(0).wait()
+            loads[3].start()
+            project(0, 0)
+            pass_on(0)
+
+    weight(5).start()
+    weight(6).start()
+    weight(7).start()
+    project(0, 1)
+    pass_on(1)
+    for b in range(1, first_q):
         weight(b).wait()
-        weight(2 * b + 3).start()
-        weight(2 * b + 4).start()
+        weight(b + SLOTS - 1).start()
 
         @pl.loop(0, 2)
         def _(j, b=b):
-            r = pl.ds(pl.multiple_of(j * half, half), half)
-            out = dot(x_s[r, :], w_s[b % SLOTS]).astype(jnp.bfloat16)
-            for h in range(STEP // HEAD):
-                piece = out[:, h * HEAD:(h + 1) * HEAD]
-                cols = pl.ds((b % nk) * STEP + h * HEAD, HEAD)
-                if b < nk:
-                    k_s[r, cols] = rotate(piece.astype(jnp.float32), cos_ref[r, :], sin_ref[r, :])
-                else:
-                    v_ref[r, cols] = piece
-                    vt_s[cols, r] = piece.T
-
-        to_far[b].start()
-        to_core[b].start()
+            project(b, j)
+
+        pass_on(b + 1)
         if b == nk - 1:
             keep_k.start()
     keep_v.start()
@@ -158,14 +178,15 @@
             keep_next.start()
             keep_x.start()
 
-        for b, turn in enumerate((2, 5, 9, 13)):
+        for turn, ready in ((1, (0, 1)), (4, (2,)), (8, (3,)), (13, (4,))):
             @pl.when(i == turn)
-            def _(b=b):
-                if b == 0:
+            def _(ready=ready):
+                if 0 in ready:
                     far_p.wait_recv()
                     relay_p.start()
-                to_far[b].wait_recv()
-                relay[b].start()
+                for n in ready:
+                    to_far[n].wait_recv()
+                    relay[n].start()
 
     for copy in (keep_p, keep_k, keep_v, keep_x, keep_next):
         copy.wait()
@@ -203,8 +224,8 @@
             pltpu.SemaphoreType.DMA((4,)),
             pltpu.SemaphoreType.DMA((SLOTS,)),
             pltpu.SemaphoreType.DMA((5,)),
-            pltpu.SemaphoreType.DMA((3 + 6 * kvw // STEP,)),
-            pltpu.SemaphoreType.DMA((3 + 6 * kvw // STEP,)),
+            pltpu.SemaphoreType.DMA((6 + 6 * kvw // STEP,)),
+            pltpu.SemaphoreType.DMA((6 + 6 * kvw // STEP,)),
         ],
         compiler_params=pltpu.CompilerParams(collective_id=0, has_side_effects=True, vmem_limit_bytes=62 * 1024 * 1024),
         cost_estimate=pl.CostEstimate(flops=2 * rows * width * (2 * kvw + qw // 2), bytes_accessed=2 * width * (rows + 2 * kvw + qw), transcendentals=0),
@@ -393,16 +414,18 @@
 def place(out, pieces, row, start):
     rows = pieces[0].shape[0]
     cols = sum(x.shape[1] for x in pieces)
-    step = 64 if cols > 1024 else rows
+    wide = cols if start % cols == 0 else math.gcd(start, cols)
+    assert wide == cols or len(pieces) == 1
+    step = 64 if cols > 4096 else rows
     per = rows // step
     return pl.pallas_call(
         place_kernel,
         out_shape=jax.ShapeDtypeStruct(out.shape, out.dtype),
         grid_spec=pltpu.PrefetchScalarGridSpec(
             num_scalar_prefetch=1,
-            grid=(per,),
-            in_specs=[*(pl.BlockSpec((step, x.shape[1]), lambda n, r: (n, 0)) for x in pieces), ANY],
-            out_specs=pl.BlockSpec((step, cols), lambda n, r: (r[0] * per + n, start // cols)),
+            grid=(per, cols // wide),
+            in_specs=[*(pl.BlockSpec((step, x.shape[1] * wide // cols), lambda n, c, r: (n, c)) for x in pieces), ANY],
+            out_specs=pl.BlockSpec((step, wide), lambda n, c, r: (r[0] * per + n, start // wide + c)),
         ),
         input_output_aliases={1 + len(pieces): 0},
         cost_estimate=pl.CostEstimate(flops=0, bytes_accessed=4 * rows * cols, transcendentals=0),
@@ -443,7 +466,8 @@
         for c, (start, cols) in enumerate(chunks):
             (_, out), other = then_send(finish, ctx, w_out, hidden, own, [p[c] for p in parts], start, cols, out)
             others.append(other)
-        out = place(out, others[:-1], send, 0)
+        out = place(out, others[:-2], send, 0)
+        out = place(out, others[-2:-1], send, CUTS[-3])
         out = place(out, others[-1:], send, CUTS[-2])
         return out, k_all[0].reshape(rows, kv, HEAD), v.reshape(rows, kv, HEAD)
 

time: 396 us -> 398 us (level)
    pallas_call x2 -> x3, Pallas kernels: 6.21 us -> 8.09 us  [place(): pl.pallas_call(place_kernel, out_shape=jax.ShapeDtypeStruct(out.shape, ou...]
where the time goes in v2:
time: 398 us; the launch traced here: 397 us
  Pallas kernels  271 us (68%)
  waiting for transfers between devices  104 us (26%)
  starting transfers between devices  13.7 us (3%)
  local copies, waits for them, and re-layouts  6.9 us (2%)
    ppermute x15, waiting for transfers between devices, then_send(): return (got, lax.ppermute(out, 'tp', swap_tp))  104 us
    pallas_call x8, Pallas kernels, project_out(): pl.pallas_call(part_kernel, out_shape=jax.ShapeDtypeStruct((rows, cols),...  62.6 us
    pallas_call x3, Pallas kernels, attention(): pl.pallas_call(functools.partial(attn_kernel, lead), out_shape=(jax.Shape...  62.6 us
    pallas_call x2, Pallas kernels, project_q(): pl.pallas_call(q_kernel, out_shape=jax.ShapeDtypeStruct((rows, width), jn...  51.8 us
    pallas_call x5, Pallas kernels, finish(): pl.pallas_call(final_kernel, out_shape=(jax.ShapeDtypeStruct((rows, cols)...  47.1 us
    pallas_call x1, Pallas kernels, front(): pl.pallas_call(front_kernel, out_shape=(jax.ShapeDtypeStruct((part, qw),...  39.2 us
    ppermute x15, starting transfers between devices, then_send(): return (got, lax.ppermute(out, 'tp', swap_tp))  13.7 us
    pallas_call x3, Pallas kernels, place(): pl.pallas_call(place_kernel, out_shape=jax.ShapeDtypeStruct(out.shape, ou...  8.09 us
  transfers between devices with their start and end apart: 15, of which 4 were waited for; matrix products, arithmetic and copies ran while one was open for 1% of the time, Pallas kernels for 50%

profile of v2, /device:TPU:0, one launch (start us, length us, event | category | flops | bytes accessed | tf_op | source)
XLA Modules:
  0.0 397.0 jit_solution(1569770438230659020)
XLA Ops:
  0.7 0.6 pad_maximum_fusion.rope_ref
  1.2 39.2 %shard_map.94 = (bf16[128,4096]{1,0:T(8,128)(2,1)}, f32[512,128]{1,0:T(8,128)}, f32[512,128]{1,0:T(8,128)}, bf16[512,512]{1,0:T(8,128)(2,1)}, bf16[128,8192]{1,0...) custom-call(bf16[512,8192]{1,0:T(8,128)(2,1)} %hid_ref.11, ...), custom_call_target="tpu_custom_call" | custom-call | flops 25769803776 | bytes 92274688 | tf_op jit(solution)/shard_map/pallas_call | solution.py:203
  40.4 17.1 %shard_map.95 = (bf16[128,4096]{1,0:T(8,128)(2,1)}, f32[128,1024]{1,0:T(8,128)}) custom-call(s32[1]{0:T(128)S(6)} %mul.23.row_ref, bf16[128,4096]{1,0:T(8,128)(2,1)} %get-tuple-element.28.q_ref.token_ref, f32[512,128]{1,0:T(8,128)} %get-tuple-element.29.cos_ref, f32[512,128]{1,0:T(8,128)} %get-tuple-element.30.sin_ref, s32[4,1,128]{2,1,0:T(1,128)} %bitcast.9, ...), custom_call_target="tpu_custom_call" | custom-call | flops 4294967296 | bytes 2097152 | tf_op jit(solution)/shard_map/pallas_call | solution.py:304
  57.5 1.5 collective-permute-start.8
  59.0 8.5 %shard_map.96.token_ref = f32[128,2048]{1,0:T(8,128)} custom-call(bf16[128,4096]{1,0:T(8,128)(2,1)} %get-tuple-element.34.x_ref, bf16[4096,8192]{1,0:T(8,128)(2,1)} %w_ref.29, f32[128,1024]{1,0:T(8,128)} %get-tuple-element.35.token_ref), custom_call_target="tpu_custom_call" | custom-call | flops 2147483648 | bytes 17825792 | tf_op jit(solution)/shard_map/pallas_call | solution.py:359
  67.5 0.5 collective-permute-start.6
  68.0 8.5 %shard_map.97.token_ref = f32[128,2048]{1,0:T(8,128)} custom-call(bf16[128,4096]{1,0:T(8,128)(2,1)} %get-tuple-element.34.x_ref, bf16[4096,8192]{1,0:T(8,128)(2,1)} %w_ref.29, f32[128,2048]{1,0:T(8,128)} %shard_map.96.token_ref), custom_call_target="tpu_custom_call" | custom-call | flops 2147483648 | bytes 17825792 | tf_op jit(solution)/shard_map/pallas_call | solution.py:359
  76.6 1.5 collective-permute-start.4
  78.1 10.3 %shard_map.98.token_ref = f32[128,2560]{1,0:T(8,128)} custom-call(bf16[128,4096]{1,0:T(8,128)(2,1)} %get-tuple-element.34.x_ref, bf16[4096,8192]{1,0:T(8,128)(2,1)} %w_ref.29, f32[128,2048]{1,0:T(8,128)} %shard_map.97.token_ref), custom_call_target="tpu_custom_call" | custom-call | flops 2684354560 | bytes 22020096 | tf_op jit(solution)/shard_map/pallas_call | solution.py:359
  88.4 3.9 shard_map.99.token_ref
  92.4 23.4 %shard_map.100.q_ref.token_ref = bf16[128,4096]{1,0:T(8,128)(2,1)} custom-call(bf16[128,8192]{1,0:T(8,128)(2,1)} %get-tuple-element.27.x_ref, bf16[8192,4096]{1,0:T(8,128)(2,1)} %w_ref.24, f32[128,512]{1,0:T(8,128)} %shard_map.99.token_ref), custom_call_target="tpu_custom_call" | custom-call | flops 8589934592 | bytes 69206016 | tf_op jit(solution)/shard_map/pallas_call | solution.py:343
  115.8 17.1 %shard_map.101 = (bf16[128,4096]{1,0:T(8,128)(2,1)}, f32[128,1024]{1,0:T(8,128)}) custom-call(s32[1]{0:T(128)S(6)} %add.17.row_ref, bf16[128,4096]{1,0:T(8,128)(2,1)} %shard_map.100.q_ref.token_ref, f32[512,128]{1,0:T(8,128)} %get-tuple-element.29.cos_ref, f32[512,128]{1,0:T(8,128)} %get-tuple-element.30.sin_ref, s32[4,1,128]{2,1,0:T(1,128)} %bitcast.10, ...), custom_call_target="tpu_custom_call" | custom-call | flops 4294967296 | bytes 2097152 | tf_op jit(solution)/shard_map/pallas_call | solution.py:304
  132.9 0.5 collective-permute-start.9
  133.4 8.5 %shard_map.102.token_ref = f32[128,2048]{1,0:T(8,128)} custom-call(bf16[128,4096]{1,0:T(8,128)(2,1)} %get-tuple-element.36.x_ref, bf16[4096,8192]{1,0:T(8,128)(2,1)} %w_ref.29, f32[128,1024]{1,0:T(8,128)} %get-tuple-element.37.token_ref), custom_call_target="tpu_custom_call" | custom-call | flops 2147483648 | bytes 17825792 | tf_op jit(solution)/shard_map/pallas_call | solution.py:359
  142.0 1.5 collective-permute-start.7
  143.5 8.5 %shard_map.103.token_ref = f32[128,2048]{1,0:T(8,128)} custom-call(bf16[128,4096]{1,0:T(8,128)(2,1)} %get-tuple-element.36.x_ref, bf16[4096,8192]{1,0:T(8,128)(2,1)} %w_ref.29, f32[128,2048]{1,0:T(8,128)} %shard_map.102.token_ref), custom_call_target="tpu_custom_call" | custom-call | flops 2147483648 | bytes 17825792 | tf_op jit(solution)/shard_map/pallas_call | solution.py:359
  152.0 10.3 %shard_map.104.token_ref = f32[128,2560]{1,0:T(8,128)} custom-call(bf16[128,4096]{1,0:T(8,128)(2,1)} %get-tuple-element.36.x_ref, bf16[4096,8192]{1,0:T(8,128)(2,1)} %w_ref.29, f32[128,2048]{1,0:T(8,128)} %shard_map.103.token_ref), custom_call_target="tpu_custom_call" | custom-call | flops 2684354560 | bytes 22020096 | tf_op jit(solution)/shard_map/pallas_call | solution.py:359
  162.3 4.0 shard_map.105.token_ref
  166.3 28.4 %shard_map.106.q_ref.token_ref = bf16[256,4096]{1,0:T(8,128)(2,1)} custom-call(bf16[256,8192]{1,0:T(8,128)(2,1)} %get-tuple-element.26.x_ref, bf16[8192,4096]{1,0:T(8,128)(2,1)} %w_ref.24, f32[128,512]{1,0:T(8,128)} %shard_map.105.token_ref), custom_call_target="tpu_custom_call" | custom-call | flops 17179869184 | bytes 71303168 | tf_op jit(solution)/shard_map/pallas_call | solution.py:343
  194.6 0.5 collective-permute-start.5
  195.2 1.5 collective-permute-start.3
  196.7 0.5 collective-permute-start.2
  197.2 28.3 %shard_map.107.x_ref = bf16[256,4096]{1,0:T(8,128)(2,1)} custom-call(s32[1]{0:T(128)S(6)} %mul.20.row_ref, bf16[256,4096]{1,0:T(8,128)(2,1)} %shard_map.106.q_ref.token_ref, f32[512,128]{1,0:T(8,128)} %get-tuple-element.29.cos_ref, f32[512,128]{1,0:T(8,128)} %get-tuple-element.30.sin_ref, s32[4,1,128]{2,1,0:T(1,128)} %bitcast.11, s32[16,128]{1,0:T(8,128)} %bitcast.7, ...), custom_call_target="tpu_custom_call" | custom-call | flops 8589934592 | bytes 4194304 | tf_op jit(solution)/shard_map/pallas_call | solution.py:304
  225.5 6.8 %shard_map.108 = (bf16[256,1024]{1,0:T(8,128)(2,1)}, bf16[512,8192]{1,0:T(8,128)(2,1)}) custom-call(s32[1]{0:T(128)} %bitcast.row_ref, bf16[256,4096]{1,0:T(8,128)(2,1)} %shard_map.107.x_ref, bf16[4096,8192]{1,0:T(8,128)(2,1)} %w_ref.29, bf16[512,8192]{1,0:T(8,128)(2,1)} %hid_ref.11, f32[128,1024]{1,0:T(8,128)} %collective-permute-done.8.pa_ref, ...), custom_call_target="tpu_custom_call" | custom-call | flops 2147483648 | bytes 10485760 | tf_op jit(solution)/shard_map/pallas_call | solution.py:385
  232.4 11.0 %shard_map.109 = (bf16[256,2048]{1,0:T(8,128)(2,1)}, bf16[512,8192]{1,0:T(8,128)(2,1)}) custom-call(s32[1]{0:T(128)} %bitcast.row_ref, bf16[256,4096]{1,0:T(8,128)(2,1)} %shard_map.107.x_ref, bf16[4096,8192]{1,0:T(8,128)(2,1)} %w_ref.29, bf16[512,8192]{1,0:T(8,128)(2,1)} %hid_ref.11, ...), custom_call_target="tpu_custom_call", output_to_operand_aliasing={{1}: (6, {})} | custom-call | flops 4294967296 | bytes 18874368 | tf_op jit(solution)/shard_map/pallas_call | solution.py:385
  243.4 11.0 %shard_map.110 = (bf16[256,2048]{1,0:T(8,128)(2,1)}, bf16[512,8192]{1,0:T(8,128)(2,1)}) custom-call(s32[1]{0:T(128)} %bitcast.row_ref, bf16[256,4096]{1,0:T(8,128)(2,1)} %shard_map.107.x_ref, bf16[4096,8192]{1,0:T(8,128)(2,1)} %w_ref.29, bf16[512,8192]{1,0:T(8,128)(2,1)} %hid_ref.11, ...), custom_call_target="tpu_custom_call", output_to_operand_aliasing={{1}: (6, {})} | custom-call | flops 4294967296 | bytes 18874368 | tf_op jit(solution)/shard_map/pallas_call | solution.py:385
  254.4 20.3 %collective-permute-done.2.pa_ref = f32[128,2560]{1,0:T(8,128)} collective-permute-done((f32[128,2560]{1,0:T(8,128)S(1)}, f32[128,2560]{1,0:T(8,128)}, u32[]{:S(2)}, u32[]{:S(2)}) %collective-permute-start.2) | collective-permute-done | bytes 1310752 | tf_op jit(solution)/shard_map/ppermute | solution.py:441
  274.7 13.2 %shard_map.111 = (bf16[256,2560]{1,0:T(8,128)(2,1)}, bf16[512,8192]{1,0:T(8,128)(2,1)}) custom-call(s32[1]{0:T(128)} %bitcast.row_ref, bf16[256,4096]{1,0:T(8,128)(2,1)} %shard_map.107.x_ref, bf16[4096,8192]{1,0:T(8,128)(2,1)} %w_ref.29, bf16[512,8192]{1,0:T(8,128)(2,1)} %hid_ref.11, ...), custom_call_target="tpu_custom_call", output_to_operand_aliasing={{1}: (6, {})} | custom-call | flops 5368709120 | bytes 23068672 | tf_op jit(solution)/shard_map/pallas_call | solution.py:385
  287.9 0.5 collective-permute-start.11
  288.4 1.5 collective-permute-start.14
  290.0 0.5 collective-permute-start.13
  290.5 1.5 collective-permute-start
  292.0 0.5 collective-permute-start.1
  292.5 77.9 %collective-permute-done.pa_ref = f32[128,512]{1,0:T(8,128)S(1)} collective-permute-done((f32[128,512]{1,0:T(8,128)S(1)}, f32[128,512]{1,0:T(8,128)S(1)}, u32[]{:S(2)}, u32[]{:S(2)}) %collective-permute-start) | collective-permute-done | bytes 262176 | tf_op jit(solution)/shard_map/ppermute | solution.py:441
  370.4 0.5 collective-permute-start.12
  370.9 5.1 %collective-permute-done.1.pb_ref = f32[128,512]{1,0:T(8,128)S(1)} collective-permute-done((f32[128,512]{1,0:T(8,128)S(1)}, f32[128,512]{1,0:T(8,128)S(1)}, u32[]{:S(2)}, u32[]{:S(2)}) %collective-permute-start.1) | collective-permute-done | bytes 262176 | tf_op jit(solution)/shard_map/ppermute | solution.py:441
  376.0 0.7 copy-done.9
  376.7 5.0 %shard_map.112 = (bf16[256,512]{1,0:T(8,128)(2,1)}, bf16[512,8192]{1,0:T(8,128)(2,1)}) custom-call(s32[1]{0:T(128)} %bitcast.row_ref, bf16[256,4096]{1,0:T(8,128)(2,1)} %shard_map.107.x_ref, bf16[4096,8192]{1,0:T(8,128)(2,1)} %w_ref.29, bf16[512,8192]{1,0:T(8,128)(2,1)} %hid_ref.11, f32[128,512]{1,0:T(8,128)} %copy-done.8, ...), custom_call_target="tpu_custom_call", output_to_operand_aliasing={{1}: (6, {})} | custom-call | flops 1073741824 | bytes 6291456 | tf_op jit(solution)/shard_map/pallas_call | solution.py:385
  381.7 0.5 collective-permute-start.10
  382.2 1.1 slice.3
  383.3 2.0 reshape.64
  385.2 0.9 reshape_squeeze.3
  386.2 0.5 collective-permute-done.12.refs_0_
  386.7 0.8 copy-done.7
  387.9 4.0 shard_map.113.refs_1_
  391.8 1.1 copy-done.2
  392.9 2.5 shard_map.114.refs_1_
  395.4 1.7 shard_map.115
  (29 shorter events, 0.4 us)
Async XLA Ops:
  57.5 137.1 %collective-permute-start.8 = (f32[128,1024]{1,0:T(8,128)}, f32[128,1024]{1,0:T(8,128)}, u32[]{:S(2)}, u32[]{:S(2)}) collective-permute-start(f32[128,1024]{1,0:T(8,128)} %get-tuple-element.35.token_ref), channel_id=1, source_target_pairs={{0,4},{4,0},{1,5},{5,1},{2,6},{6,2},{3,7},{7,3}} | collective-permute-start | bytes 1572872 | tf_op jit(solution)/shard_map/ppermute | solution.py:441
  67.5 129.2 %collective-permute-start.6 = (f32[128,2048]{1,0:T(8,128)}, f32[128,2048]{1,0:T(8,128)}, u32[]{:S(2)}, u32[]{:S(2)}) collective-permute-start(f32[128,2048]{1,0:T(8,128)} %shard_map.96.token_ref), channel_id=1, source_target_pairs={{0,4},{4,0},{1,5},{5,1},{2,6},{6,2},{3,7},{7,3}} | collective-permute-start | bytes 3145736 | tf_op jit(solution)/shard_map/ppermute | solution.py:441
  76.6 166.8 %collective-permute-start.4 = (f32[128,2048]{1,0:T(8,128)}, f32[128,2048]{1,0:T(8,128)}, u32[]{:S(2)}, u32[]{:S(2)}) collective-permute-start(f32[128,2048]{1,0:T(8,128)} %shard_map.97.token_ref), channel_id=1, source_target_pairs={{0,4},{4,0},{1,5},{5,1},{2,6},{6,2},{3,7},{7,3}} | collective-permute-start | bytes 3145736 | tf_op jit(solution)/shard_map/ppermute | solution.py:441
  132.9 62.2 %collective-permute-start.9 = (f32[128,1024]{1,0:T(8,128)}, f32[128,1024]{1,0:T(8,128)S(1)}, u32[]{:S(2)}, u32[]{:S(2)}) collective-permute-start(f32[128,1024]{1,0:T(8,128)} %get-tuple-element.37.token_ref), channel_id=1, source_target_pairs={{0,4},{4,0},{1,5},{5,1},{2,6},{6,2},{3,7},{7,3}} | collective-permute-start | bytes 1572872 | tf_op jit(solution)/shard_map/ppermute | solution.py:441
  142.0 90.4 %collective-permute-start.7 = (f32[128,2048]{1,0:T(8,128)}, f32[128,2048]{1,0:T(8,128)}, u32[]{:S(2)}, u32[]{:S(2)}) collective-permute-start(f32[128,2048]{1,0:T(8,128)} %shard_map.102.token_ref), channel_id=1, source_target_pairs={{0,4},{4,0},{1,5},{5,1},{2,6},{6,2},{3,7},{7,3}} | collective-permute-start | bytes 3145736 | tf_op jit(solution)/shard_map/ppermute | solution.py:441
  166.3 28.9 %copy-start.1 = (f32[128,2560]{1,0:T(8,128)S(1)}, f32[128,2560]{1,0:T(8,128)}, u32[]{:S(2)}) copy-start(f32[128,2560]{1,0:T(8,128)} %shard_map.104.token_ref) | copy-start | bytes 3932164
  166.3 30.4 %copy-start = (f32[128,2560]{1,0:T(8,128)S(1)}, f32[128,2560]{1,0:T(8,128)}, u32[]{:S(2)}) copy-start(f32[128,2560]{1,0:T(8,128)} %shard_map.98.token_ref) | copy-start | bytes 3932164
  194.6 48.7 %collective-permute-start.5 = (f32[128,2048]{1,0:T(8,128)}, f32[128,2048]{1,0:T(8,128)}, u32[]{:S(2)}, u32[]{:S(2)}) collective-permute-start(f32[128,2048]{1,0:T(8,128)} %shard_map.103.token_ref), channel_id=1, source_target_pairs={{0,4},{4,0},{1,5},{5,1},{2,6},{6,2},{3,7},{7,3}} | collective-permute-start | bytes 3145736 | tf_op jit(solution)/shard_map/ppermute | solution.py:441
  195.2 30.4 %copy-start.6 = (f32[128,1024]{1,0:T(8,128)}, f32[128,1024]{1,0:T(8,128)S(1)}, u32[]{:S(2)}) copy-start(f32[128,1024]{1,0:T(8,128)S(1)} %collective-permute-done.9.pb_ref) | copy-start | bytes 1572868
  195.2 59.2 %collective-permute-start.3 = (f32[128,2560]{1,0:T(8,128)S(1)}, f32[128,2560]{1,0:T(8,128)}, u32[]{:S(2)}, u32[]{:S(2)}) collective-permute-start(f32[128,2560]{1,0:T(8,128)S(1)} %copy-done.1), channel_id=1, source_target_pairs={{0,4},{4,0},{1,5},{5,1},{2,6},{6,2},{3,7},{7,3}} | collective-permute-start | bytes 3932168 | tf_op jit(solution)/shard_map/ppermute | solution.py:441
  196.7 78.0 %collective-permute-start.2 = (f32[128,2560]{1,0:T(8,128)S(1)}, f32[128,2560]{1,0:T(8,128)}, u32[]{:S(2)}, u32[]{:S(2)}) collective-permute-start(f32[128,2560]{1,0:T(8,128)S(1)} %copy-done), channel_id=1, source_target_pairs={{0,4},{4,0},{1,5},{5,1},{2,6},{6,2},{3,7},{7,3}} | collective-permute-start | bytes 3932168 | tf_op jit(solution)/shard_map/ppermute | solution.py:441
  274.7 15.8 %copy-start.3 = (f32[128,512]{1,0:T(8,128)S(1)}, f32[128,512]{1,0:T(8,128)}, u32[]{:S(2)}) copy-start(f32[128,512]{1,0:T(8,128)} %shard_map.99.token_ref) | copy-start | bytes 786436
  274.7 17.3 %copy-start.4 = (f32[128,512]{1,0:T(8,128)S(1)}, f32[128,512]{1,0:T(8,128)}, u32[]{:S(2)}) copy-start(f32[128,512]{1,0:T(8,128)} %shard_map.105.token_ref) | copy-start | bytes 786436
  287.9 103.9 %collective-permute-start.11 = (bf16[256,2560]{1,0:T(8,128)(2,1)}, bf16[256,2560]{1,0:T(8,128)(2,1)S(1)}, u32[]{:S(2)}, u32[]{:S(2)}) collective-permute-start(bf16[256,2560]{1,0:T(8,128)(2,1)} %get-tuple-element.43), channel_id=1, source_target_pairs={{0,4},{4,0},{1,5},{5,1},{2,6},{6,2},{3,7},{7,3}} | collective-permute-start | bytes 3932168 | tf_op jit(solution)/shard_map/ppermute | solution.py:441
  288.4 98.3 %collective-permute-start.14 = (bf16[256,2048]{1,0:T(8,128)(2,1)}, bf16[256,2048]{1,0:T(8,128)(2,1)S(1)}, u32[]{:S(2)}, u32[]{:S(2)}) collective-permute-start(bf16[256,2048]{1,0:T(8,128)(2,1)} %get-tuple-element.46), channel_id=1, source_target_pairs={{0,4},{4,0},{1,5},{5,1},{2,6},{6,2},{3,7},{7,3}} | collective-permute-start | bytes 3145736 | tf_op jit(solution)/shard_map/ppermute | solution.py:441
  290.0 96.7 %collective-permute-start.13 = (bf16[256,2048]{1,0:T(8,128)(2,1)}, bf16[256,2048]{1,0:T(8,128)(2,1)}, u32[]{:S(2)}, u32[]{:S(2)}) collective-permute-start(bf16[256,2048]{1,0:T(8,128)(2,1)} %get-tuple-element.45), channel_id=1, source_target_pairs={{0,4},{4,0},{1,5},{5,1},{2,6},{6,2},{3,7},{7,3}} | collective-permute-start | bytes 3145736 | tf_op jit(solution)/shard_map/ppermute | solution.py:441
  290.5 79.9 %collective-permute-start = (f32[128,512]{1,0:T(8,128)S(1)}, f32[128,512]{1,0:T(8,128)S(1)}, u32[]{:S(2)}, u32[]{:S(2)}) collective-permute-start(f32[128,512]{1,0:T(8,128)S(1)} %copy-done.3), channel_id=1, source_target_pairs={{0,4},{4,0},{1,5},{5,1},{2,6},{6,2},{3,7},{7,3}} | collective-permute-start | bytes 786440 | tf_op jit(solution)/shard_map/ppermute | solution.py:441
  292.0 84.0 %collective-permute-start.1 = (f32[128,512]{1,0:T(8,128)S(1)}, f32[128,512]{1,0:T(8,128)S(1)}, u32[]{:S(2)}, u32[]{:S(2)}) collective-permute-start(f32[128,512]{1,0:T(8,128)S(1)} %copy-done.4), channel_id=1, source_target_pairs={{0,4},{4,0},{1,5},{5,1},{2,6},{6,2},{3,7},{7,3}} | collective-permute-start | bytes 786440 | tf_op jit(solution)/shard_map/ppermute | solution.py:441
  370.4 5.6 %copy-start.8 = (f32[128,512]{1,0:T(8,128)}, f32[128,512]{1,0:T(8,128)S(1)}, u32[]{:S(2)}) copy-start(f32[128,512]{1,0:T(8,128)S(1)} %collective-permute-done.pa_ref) | copy-start | bytes 786436
  370.4 16.3 %collective-permute-start.12 = (bf16[256,1024]{1,0:T(8,128)(2,1)}, bf16[256,1024]{1,0:T(8,128)(2,1)S(1)}, u32[]{:S(2)}, u32[]{:S(2)}) collective-permute-start(bf16[256,1024]{1,0:T(8,128)(2,1)} %get-tuple-element.44), channel_id=1, source_target_pairs={{0,4},{4,0},{1,5},{5,1},{2,6},{6,2},{3,7},{7,3}} | collective-permute-start | bytes 1572872 | tf_op jit(solution)/shard_map/ppermute | solution.py:441
  376.0 0.7 copy-start.9
  381.7 13.7 %collective-permute-start.10 = (bf16[256,512]{1,0:T(8,128)(2,1)}, bf16[256,512]{1,0:T(8,128)(2,1)}, u32[]{:S(2)}, u32[]{:S(2)}) collective-permute-start(bf16[256,512]{1,0:T(8,128)(2,1)} %get-tuple-element.42), channel_id=1, source_target_pairs={{0,4},{4,0},{1,5},{5,1},{2,6},{6,2},{3,7},{7,3}} | collective-permute-start | bytes 786440 | tf_op jit(solution)/shard_map/ppermute | solution.py:441
  386.7 0.8 copy-start.7
  386.7 1.2 copy-start.5
  391.8 1.1 copy-start.2
